TPU v7x, 256 devices: a whole 4x4x8 slice. The times are simulated.
256 devices in a mesh: space: 32 (over x, z_hi, core), mem: 8 (over y, z_lo).
Axes of the slice: x: 4, y: 4, z: 8 (z_hi: 4, z_lo: 2; z = z_hi * 2 + z_lo), core: 2. Of those that a mesh axis runs over, the one named last changes fastest.
Arguments:
- ensemble: bfloat16 [32, 32, 512, 1536], P('mem', None, 'space'), may hold values from -12 to 12
- vector: bfloat16 [32, 512, 1536], P(None, 'space'), may hold values from -6 to 6
- modes: float32 [16, 32], replicated, may hold values from -1 to 1
- legendre: bfloat16 [512, 512, 256], P('space'), may hold values from -0.25 to 0.25
- spectrum: float32 [512, 256], P('space'), may hold values from 0.1 to 1
- truncation: int32 [1], replicated, may hold values from 543 to 702
Outputs:
- covariance_apply: bfloat16 [32, 512, 1536], P(None, 'space')
All inputs are finite; a program needn't handle non-finite values.
Results may differ from a plain program's by a relative error of at most 0.014.
Values may be sent and summed in bfloat16 or wider, within the bound.
No kernel may reach another device: no remote copies, remote signals or barrier semaphores. Data moves between devices by JAX's collectives and lax.ppermute only.
A program may use at most 128 MiB of HBM per device.

v0:
```python
import functools
import math

import jax
import jax.numpy as jnp
import numpy as np
from jax import lax
from jax.experimental import pallas as pl
from jax.experimental.pallas import tpu as pltpu
from jax.sharding import Mesh
from jax.sharding import PartitionSpec as P


NLON = 1536
M = 512
SPACE = ("space_0", "space_1", "space_2")
F32 = jnp.float32
BF16 = jnp.bfloat16
NT = (((1,), (1,)), ((), ()))
TN = (((0,), (0,)), ((), ()))


def angle_tables(block):
    points = np.arange(NLON)[None, :]
    amplitude = math.sqrt(2.0 / NLON)

    def angles(waves):
        return (points * waves[:, None] % NLON) * (2.0 * math.pi / NLON)

    low = angles(np.arange(block))
    high = angles(np.arange(M // block) * block)
    tables = (np.cos(low) * amplitude, np.sin(low) * amplitude, np.cos(high), np.sin(high))
    return [jnp.asarray(t, F32) for t in tables]


def iota2(shape, dim):
    return lax.broadcasted_iota(jnp.int32, shape, dim)


def one_hot(match):
    return jnp.where(match, 1.0, 0.0).astype(BF16)


def build_table(ft_ref, low_c, low_s, high_c, high_s):
    block = low_c.shape[0]

    def build(t, carry):
        hc = high_c[pl.ds(t, 1), :]
        hs = high_s[pl.ds(t, 1), :]
        at = pl.multiple_of(t * block, block)
        ft_ref[pl.ds(at, block), :] = (low_c[...] * hc - low_s[...] * hs).astype(BF16)
        ft_ref[pl.ds(M + at, block), :] = -(low_s[...] * hc + low_c[...] * hs).astype(BF16)
        return carry

    lax.fori_loop(0, M // block, build, 0)


def forward_kernel(modes_ref, low_c, low_s, high_c, high_s, e_ref, v_ref, z_ref, ft_ref, kp, p, y):
    k = pl.program_id(0)
    members = pl.num_programs(0)
    modes_n, levels = modes_ref.shape
    rows = kp.shape[0] // modes_n
    fields = p.shape[0] // rows

    @pl.when(k == 0)
    def _():
        ra = one_hot(iota2((rows * modes_n, modes_n), 0) % modes_n == iota2((rows * modes_n, modes_n), 1))
        la = one_hot(iota2((levels, levels * rows), 1) // rows == iota2((levels, levels * rows), 0))
        spread_rows = jnp.dot(ra, modes_ref[...].astype(BF16), preferred_element_type=F32)
        full = jnp.dot(spread_rows.astype(BF16), la, preferred_element_type=F32)
        mask = iota2(kp.shape, 0) // modes_n == iota2(kp.shape, 1) % rows
        kp[...] = jnp.where(mask, full, 0.0).astype(BF16)

        build_table(ft_ref, low_c, low_s, high_c, high_s)

    product = e_ref[0] * v_ref[...]
    projected = jnp.dot(kp[...], product, preferred_element_type=F32).astype(BF16)
    for a in range(rows):
        at = pl.multiple_of(a * fields + k * modes_n, modes_n)
        p[pl.ds(at, modes_n), :] = projected[a * modes_n : (a + 1) * modes_n]

    @pl.when(k == members - 1)
    def _():
        lane = iota2((M, 2 * fields), 1)
        for chunk in range(rows // 4):
            wide = 4 * fields
            got = lax.dot_general(
                ft_ref[...], p[chunk * wide : (chunk + 1) * wide, :], NT, preferred_element_type=F32
            )
            for pair in range(2):
                lanes = slice(pair * 2 * fields, (pair + 1) * 2 * fields)
                tc = got[:M, lanes]
                ts = got[M:, lanes]
                a = chunk * 4 + pair * 2
                y[pl.ds(a, M, stride=rows), :] = jnp.where(lane < fields, tc, pltpu.roll(ts, fields, 1))
                y[pl.ds(a + 1, M, stride=rows), :] = jnp.where(lane < fields, pltpu.roll(tc, fields, 1), ts)

        z_ref[...] = y[...].astype(BF16)


def forward(modes, ensemble, vector):
    members, levels, rows, lons = ensemble.shape
    modes_n = modes.shape[0]
    fields = members * modes_n
    low_c, low_s, high_c, high_s = angle_tables(16)
    whole = lambda s: pl.BlockSpec(s, lambda k: (0,) * len(s))
    return pl.pallas_call(
        forward_kernel,
        grid=(members,),
        in_specs=[
            whole(modes.shape),
            whole(low_c.shape),
            whole(low_s.shape),
            whole(high_c.shape),
            whole(high_s.shape),
            pl.BlockSpec((1, levels * rows, lons), lambda k: (k, 0, 0)),
            whole((levels * rows, lons)),
        ],
        out_specs=whole((M * rows, 2 * fields)),
        out_shape=jax.ShapeDtypeStruct((M * rows, 2 * fields), BF16),
        scratch_shapes=[
            pltpu.VMEM((2 * M, lons), BF16),
            pltpu.VMEM((rows * modes_n, levels * rows), BF16),
            pltpu.VMEM((rows * fields, lons), BF16),
            pltpu.VMEM((M * rows, 2 * fields), F32),
        ],
        compiler_params=pltpu.CompilerParams(vmem_limit_bytes=62 * 2**20),
        name="forward",
    )(
        modes,
        low_c,
        low_s,
        high_c,
        high_s,
        ensemble.reshape(members, levels * rows, lons),
        vector.reshape(levels * rows, lons),
    )


def divide_kernel(scalars, low_c, low_s, high_c, high_s, e_ref, *rest, rows):
    *out_refs, ft_ref, perm = rest
    parts = len(out_refs)
    share = out_refs[0].shape[1]
    own = scalars[2]

    @pl.when(pl.program_id(0) == 0)
    def _():
        build_table(ft_ref, low_c, low_s, high_c, high_s)
        row = iota2(perm.shape, 0)
        col = iota2(perm.shape, 1)
        per = rows // parts
        part = (own + row // share) % parts
        level = row % share // per
        lat = part * per + row % per
        perm[...] = one_hot(col == level * rows + lat)

    moved = jnp.dot(perm[...], e_ref[0], preferred_element_type=F32).astype(BF16)
    for d, out_ref in enumerate(out_refs):
        out_ref[0] = moved[d * share : (d + 1) * share]


def divide(scalars, ensemble, parts):
    members, levels, rows, lons = ensemble.shape
    share = levels * rows // parts
    tables = angle_tables(16)
    return pl.pallas_call(
        functools.partial(divide_kernel, rows=rows),
        grid_spec=pltpu.PrefetchScalarGridSpec(
            num_scalar_prefetch=1,
            grid=(members,),
            in_specs=[pl.BlockSpec(t.shape, lambda k, _: (0, 0)) for t in tables]
            + [pl.BlockSpec((1, levels * rows, lons), lambda k, _: (k, 0, 0))],
            out_specs=[pl.BlockSpec((1, share, lons), lambda k, _: (k, 0, 0))] * parts
            + [pl.BlockSpec((2 * M, lons), lambda k, _: (0, 0))],
            scratch_shapes=[pltpu.VMEM((levels * rows, levels * rows), BF16)],
        ),
        out_shape=[jax.ShapeDtypeStruct((members, share, lons), BF16)] * parts
        + [jax.ShapeDtypeStruct((2 * M, lons), BF16)],
        compiler_params=pltpu.CompilerParams(vmem_limit_bytes=62 * 2**20),
        cost_estimate=pl.CostEstimate(flops=10**10, bytes_accessed=2 * 10**7, transcendentals=0),
        name="divide",
    )(scalars, *tables, ensemble.reshape(members, levels * rows, lons))


def spectral_kernel(scalars, spectrum_ref, x_ref, l_hbm, out_ref, s, l_all, arrive):
    step = pl.program_id(0)
    sources, per, rows, lanes = x_ref.shape
    waves = l_all.shape[0]
    degrees = l_all.shape[2]

    def load(at):
        part = pl.ds(at * per, per)
        return pltpu.make_async_copy(l_hbm.at[part], l_all.at[part], arrive.at[at])

    @pl.when(step == 0)
    def _():
        for at in range(waves // per):
            load(at).start()

    load(step).wait()
    for i in range(per):
        m = step * per + i
        x = x_ref[:, i].reshape(sources * rows, lanes)
        harmonic = lax.dot_general(x, l_all[m], TN, preferred_element_type=F32)
        total = scalars[1] + m + iota2((1, degrees), 1)
        factor = jnp.where(total <= scalars[0], spectrum_ref[pl.ds(m, 1), :], 0.0)
        weighted = (harmonic * factor).astype(BF16)
        back = lax.dot_general(l_all[m], weighted, NT, preferred_element_type=F32)
        s[pl.ds(m, sources * rows, stride=waves), :] = back

    @pl.when(step == pl.num_programs(0) - 1)
    def _():
        out_ref[...] = s[...].astype(BF16)


def spectral(scalars, spectrum, arrived, legendre):
    sources, waves, rows, lanes = arrived.shape
    lats, degrees = legendre.shape[1:]
    per = 4
    return pl.pallas_call(
        spectral_kernel,
        grid_spec=pltpu.PrefetchScalarGridSpec(
            num_scalar_prefetch=1,
            grid=(waves // per,),
            in_specs=[
                pl.BlockSpec((waves, degrees), lambda i, _: (0, 0)),
                pl.BlockSpec((sources, per, rows, lanes), lambda i, _: (0, i, 0, 0)),
                pl.BlockSpec(memory_space=pltpu.MemorySpace.HBM),
            ],
            out_specs=pl.BlockSpec((sources * rows * waves, lanes), lambda i, _: (0, 0)),
            scratch_shapes=[
                pltpu.VMEM((sources * rows * waves, lanes), F32),
                pltpu.VMEM((waves, lats, degrees), BF16),
                pltpu.SemaphoreType.DMA((waves // per,)),
            ],
        ),
        out_shape=jax.ShapeDtypeStruct((sources * rows * waves, lanes), BF16),
        compiler_params=pltpu.CompilerParams(vmem_limit_bytes=62 * 2**20),
        name="spectral",
    )(scalars, spectrum, arrived, legendre)


def backward_kernel(scalars, modes_ref, r_ref, ft_ref, *rest):
    *e_refs, out_ref, kl, g = rest
    modes_n, levels = modes_ref.shape
    sources, parts, rows, waves, lanes = r_ref.shape
    members = e_refs[0].shape[0]
    fields = members * modes_n
    share = levels * rows
    columns = rows * modes_n

    @pl.when(pl.program_id(0) == 0)
    def _():
        height, width = kl.shape
        la = one_hot(iota2((height, levels), 0) % share // rows == iota2((height, levels), 1))
        ra = one_hot(iota2((modes_n, width), 1) % modes_n == iota2((modes_n, width), 0))
        spread_rows = lax.dot_general(la, modes_ref[...].astype(BF16), NT, preferred_element_type=F32)
        full = jnp.dot(spread_rows.astype(BF16), ra, preferred_element_type=F32)
        row = iota2(kl.shape, 0)
        col = iota2(kl.shape, 1)
        mask = (row // share == col // columns) & (row % rows == col % columns // modes_n)
        kl[...] = jnp.where(mask, full, 0.0).astype(BF16)
        for d in range(parts):
            source = (scalars[2] + parts - d) % parts
            for a in range(rows):
                flipped = r_ref[:, source, a].reshape(sources * waves, lanes).T
                for r in range(2):
                    for k in range(members):
                        at = r * fields + k * modes_n
                        to = (d * members + k) * columns + a * modes_n
                        g[to : to + modes_n, r * M : (r + 1) * M] = flipped[at : at + modes_n]

    spread = jnp.dot(g[...], ft_ref[...], preferred_element_type=F32).astype(BF16)
    group = members * columns
    total = None
    for d in range(parts):
        lifted = jnp.dot(kl[...], spread[d * group : (d + 1) * group], preferred_element_type=F32)
        for k in range(members):
            term = e_refs[d][k].astype(F32) * lifted[k * share : (k + 1) * share]
            total = term if total is None else total + term
    out_ref[...] = total.astype(BF16)


def backward(scalars, modes, returned, fourier, pieces):
    _, parts, rows, _, _ = returned.shape
    members, share, lons = pieces[0].shape
    modes_n = modes.shape[0]
    chunk = 256
    columns = members * rows * modes_n
    return pl.pallas_call(
        backward_kernel,
        grid_spec=pltpu.PrefetchScalarGridSpec(
            num_scalar_prefetch=1,
            grid=(lons // chunk,),
            in_specs=[
                pl.BlockSpec(modes.shape, lambda i, _: (0, 0)),
                pl.BlockSpec(returned.shape, lambda i, _: (0, 0, 0, 0, 0)),
                pl.BlockSpec((2 * M, chunk), lambda i, _: (0, i)),
            ]
            + [pl.BlockSpec((members, share, chunk), lambda i, _: (0, 0, i))] * parts,
            out_specs=pl.BlockSpec((share, chunk), lambda i, _: (0, i)),
            scratch_shapes=[
                pltpu.VMEM((members * share, columns), BF16),
                pltpu.VMEM((parts * columns, 2 * M), BF16),
            ],
        ),
        out_shape=jax.ShapeDtypeStruct((share, lons), BF16),
        compiler_params=pltpu.CompilerParams(vmem_limit_bytes=62 * 2**20),
        name="backward",
    )(scalars, modes, returned, fourier, *pieces)


def place_kernel(x_ref, out_ref, perm, *, levels):
    parts, halves, share, chunk = x_ref.shape
    height = perm.shape[0]

    @pl.when(pl.program_id(0) == 0)
    def _():
        rows = height // levels
        row = iota2(perm.shape, 0)
        level = row // rows
        lat = row % rows
        per = rows // parts
        half = levels // halves
        wanted = (lat // per * halves + level // half) * share + level % half * per + lat % per
        perm[...] = one_hot(iota2(perm.shape, 1) == wanted)

    x = x_ref[...].reshape(height, chunk)
    out_ref[...] = jnp.dot(perm[...], x, preferred_element_type=F32).astype(BF16)


def place(gathered, levels):
    parts, halves, share, lons = gathered.shape
    chunk = 256
    height = parts * halves * share
    return pl.pallas_call(
        functools.partial(place_kernel, levels=levels),
        grid=(lons // chunk,),
        in_specs=[pl.BlockSpec((parts, halves, share, chunk), lambda i: (0, 0, 0, i))],
        out_specs=pl.BlockSpec((height, chunk), lambda i: (0, i)),
        out_shape=jax.ShapeDtypeStruct((height, lons), BF16),
        scratch_shapes=[pltpu.VMEM((height, height), BF16)],
        compiler_params=pltpu.CompilerParams(vmem_limit_bytes=62 * 2**20),
        name="place",
    )(gathered)


def swap(blocks, axes):
    return lax.all_to_all(blocks, axes, 0, 0, tiled=True)


def on_device(ensemble, vector, modes, legendre, spectrum, truncation):
    members, levels, rows, lons = ensemble.shape
    waves = legendre.shape[0]
    sources = lax.axis_size(SPACE)
    parts = lax.axis_size("mem_y")
    halves = lax.axis_size("mem_z")
    lanes = 2 * members * modes.shape[0]
    quarter = rows // parts
    first_wave = lax.axis_index(SPACE) * waves
    scalars = jnp.stack([truncation[0], first_wave.astype(jnp.int32), lax.axis_index("mem_y").astype(jnp.int32)])
    zonal = forward(modes, ensemble, vector)
    arrived = swap(zonal.reshape(sources, waves, rows, lanes), SPACE)
    held, _ = lax.optimization_barrier((ensemble, zonal))
    *pieces, fourier = divide(scalars, held, parts)
    for d in range(1, parts):
        pieces[d] = lax.ppermute(pieces[d], "mem_y", [(i, (i + d) % parts) for i in range(parts)])
    synthesis = spectral(scalars, spectrum, arrived, legendre)
    returned = swap(synthesis.reshape(sources * parts, quarter, waves, lanes), SPACE + ("mem_y",))
    partial_value = backward(scalars, modes, returned.reshape(sources, parts, quarter, waves, lanes), fourier, pieces)
    blocks = swap(partial_value.reshape(halves, -1, lons), "mem_z")
    share = jnp.sum(blocks.astype(F32), axis=0)
    rounded = (share / (members * parts * halves - 1)).astype(BF16)
    everyone = jnp.broadcast_to(rounded[None], (parts * halves, *rounded.shape))
    gathered = swap(everyone, ("mem_y", "mem_z"))
    return place(gathered.reshape(parts, halves, -1, lons), levels).reshape(levels, rows, lons)


def solution(mesh):
    torus = Mesh(
        mesh.devices.reshape(4, 4, 2, 4, 2), ("space_0", "space_1", "space_2", "mem_y", "mem_z")
    )
    in_specs = (
        P(("mem_y", "mem_z"), None, SPACE, None),
        P(None, SPACE, None),
        P(),
        P(SPACE, None, None),
        P(SPACE, None),
        P(),
    )
    out_specs = P(None, SPACE, None)
    return jax.shard_map(on_device, mesh=torus, in_specs=in_specs, out_specs=out_specs, check_vma=False)
```

profile of v0, /device:TPU:2, one launch (start us, length us, event | category | flops | bytes accessed | tf_op | source)
XLA Modules:
  0.0 244.3 jit_solution(14696357752008051562)
XLA Ops:
  0.0 12.9 %forward.1 = bf16[8192,128]{1,0:T(8,128)(2,1)} custom-call(f32[16,32]{1,0:T(8,128)} %modes_ref.3, f32[16,1536]{1,0:T(8,128)} %constant.36.clone.low_c, f32[16,1536]{1,0:T(8,128)} %constant.37.clone.low_s, f32[32,1536]{1,0:T(8,128)} %constant.38.clone.high_c, f32[32,1536]{1,0:T(8,128)} %constant.39.clone.high_s, bf16[4,512,1536]{2,1,0:T(8,128)(2,1)} %bitcast.13, ...), custom_call_target="tpu_custom_call" | custom-call | tf_op jit(solution)/shard_map/forward/pallas_call | solution.py:107
  12.9 11.7 %all-to-all-start = ((bf16[32,16,16,128]{3,2,1,0:T(8,128)(2,1)}), bf16[32,16,16,128]{3,2,1,0:T(8,128)(2,1)}, u32[]{:S(2)}, u32[]{:S(2)}) async-start(bf16[32,16,16,128]{3,2,1,0:T(8,128)(2,1)} %bitcast.11), calls=%async_computation | async-start | bytes 4194304 | tf_op jit(solution)/shard_map/all_to_all | solution.py:349
  25.2 0.7 pad_add_fusion.scalars
  25.9 47.1 %all-to-all-done.x_ref = bf16[32,16,16,128]{3,2,1,0:T(8,128)(2,1)} async-done(((bf16[32,16,16,128]{3,2,1,0:T(8,128)(2,1)}), bf16[32,16,16,128]{3,2,1,0:T(8,128)(2,1)}, u32[]{:S(2)}, u32[]{:S(2)}) %all-to-all-start) | async-done | bytes 2097184 | tf_op jit(solution)/shard_map/all_to_all | solution.py:349
  73.0 8.6 %spectral.1 = bf16[8192,128]{1,0:T(8,128)(2,1)} custom-call(s32[3]{0:T(128)} %pad_add_fusion.scalars, f32[16,256]{1,0:T(8,128)} %spectrum_ref.1, bf16[32,16,16,128]{3,2,1,0:T(8,128)(2,1)} %all-to-all-done.x_ref, bf16[16,512,256]{2,1,0:T(8,128)(2,1)} %l_hbm.1), custom_call_target="tpu_custom_call" | custom-call | tf_op jit(solution)/shard_map/spectral/pallas_call | solution.py:220
  81.6 12.6 %all-to-all-start.1 = ((bf16[128,4,16,128]{3,2,1,0:T(8,128)(2,1)}), bf16[128,4,16,128]{3,2,1,0:T(8,128)(2,1)}, u32[]{:S(2)}, u32[]{:S(2)}) async-start(bf16[128,4,16,128]{3,2,1,0:T(8,128)(2,1)} %bitcast.12), calls=%async_computation.1 | async-start | bytes 4194304 | tf_op jit(solution)/shard_map/all_to_all | solution.py:349
  94.2 10.8 %divide.1 = (bf16[4,128,1536]{2,1,0:T(8,128)(2,1)}, bf16[4,128,1536]{2,1,0:T(8,128)(2,1)}, bf16[4,128,1536]{2,1,0:T(8,128)(2,1)}, bf16[4,128,1536]{2,1,0:T(8,128)(2,1)}, bf16[1024,1536]{1,0:T(8,128)(2,1)}) custom-call(s32[3]{0:T(128)} %pad_add_fusion.scalars, f32[16,1536]{1,0:T(8,128)} %constant.36.clone.low_c, f32[16,1536]{1,0:T(8,128)} %constant.37.clone.low_s, ...), custom_call_target="tpu_custom_call" | custom-call | flops 10000000000 | bytes 20000000 | tf_op jit(solution)/shard_map/divide/pallas_call | solution.py:166
  105.0 1.5 collective-permute-start
  106.5 2.7 %collective-permute-start.1 = (bf16[4,128,1536]{2,1,0:T(8,128)(2,1)}, bf16[4,128,1536]{2,1,0:T(8,128)(2,1)}, u32[]{:S(2)}, u32[]{:S(2)}) collective-permute-start(bf16[4,128,1536]{2,1,0:T(8,128)(2,1)} %get-tuple-element.15), channel_id=1, source_target_pairs={{0,4},{2,6},{4,0},{6,2},{1,5},{3,7},{5,1},{7,3},{8,12},{10,14},{12... | collective-permute-start | bytes 4718600 | tf_op jit(solution)/shard_map/ppermute | solution.py:367
  109.2 1.5 collective-permute-start.2
  110.7 46.0 %collective-permute-done.rest_1_ = bf16[4,128,1536]{2,1,0:T(8,128)(2,1)S(1)} collective-permute-done((bf16[4,128,1536]{2,1,0:T(8,128)(2,1)}, bf16[4,128,1536]{2,1,0:T(8,128)(2,1)S(1)}, u32[]{:S(2)}, u32[]{:S(2)}) %collective-permute-start) | collective-permute-done | bytes 1572896 | tf_op jit(solution)/shard_map/ppermute | solution.py:367
  156.7 0.0 copy-start
  156.7 34.9 %collective-permute-done.1.rest_2_ = bf16[4,128,1536]{2,1,0:T(8,128)(2,1)} collective-permute-done((bf16[4,128,1536]{2,1,0:T(8,128)(2,1)}, bf16[4,128,1536]{2,1,0:T(8,128)(2,1)}, u32[]{:S(2)}, u32[]{:S(2)}) %collective-permute-start.1) | collective-permute-done | bytes 1572896 | tf_op jit(solution)/shard_map/ppermute | solution.py:367
  191.6 0.0 collective-permute-done.2.rest_3_
  191.6 0.0 all-to-all-done.1
  191.6 0.0 copy-done
  191.6 13.0 %backward.1 = bf16[128,1536]{1,0:T(8,128)(2,1)} custom-call(s32[3]{0:T(128)} %pad_add_fusion.scalars, f32[16,32]{1,0:T(8,128)} %modes_ref.3, bf16[32,4,4,16,128]{4,3,2,1,0:T(8,128)(2,1)} %bitcast.6.r_ref, bf16[1024,1536]{1,0:T(8,128)(2,1)} %get-tuple-element.12.ft_ref, bf16[4,128,1536]{2,1,0:T(8,128)(2,1)} %get-tuple-element.13.rest_0_, ...), custom_call_target="tpu_custom_call" | custom-call | tf_op jit(solution)/shard_map/backward/pallas_call | solution.py:290
  204.6 9.9 %all_to_all.20 = bf16[2,64,1536]{2,1,0:T(8,128)(2,1)S(1)} all-to-all(bf16[2,64,1536]{2,1,0:T(8,128)(2,1)} %bitcast.17), channel_id=1, replica_groups=mesh['space_0'=4,'space_1'=4,'space_2'=2,'mem_y'=4,'mem_z'=2] {'mem_z'}, dimensions={0} | all-to-all | bytes 786432 | tf_op jit(solution)/shard_map/all_to_all | solution.py:349
  214.5 0.1 convert_reduce_fusion
  214.6 0.1 broadcast_in_dim.2
  214.8 24.1 %all_to_all.21 = bf16[8,64,1536]{2,1,0:T(8,128)(2,1)} all-to-all(bf16[8,64,1536]{2,1,0:T(8,128)(2,1)S(1)} %broadcast_in_dim.2), channel_id=1, replica_groups=mesh['space_0'=4,'space_1'=4,'space_2'=2,'mem_y'=4,'mem_z'=2] {'mem_y','..., dimensions={0} | all-to-all | bytes 3145728 | tf_op jit(solution)/shard_map/all_to_all | solution.py:349
  238.8 5.5 %place.1 = bf16[512,1536]{1,0:T(8,128)(2,1)} custom-call(bf16[4,2,64,1536]{3,2,1,0:T(8,128)(2,1)} %bitcast.15), custom_call_target="tpu_custom_call" | custom-call | tf_op jit(solution)/shard_map/place/pallas_call | solution.py:336
  (1 shorter events, 0.0 us)
Async XLA Ops:
  12.9 60.1 %all-to-all-start = ((bf16[32,16,16,128]{3,2,1,0:T(8,128)(2,1)}), bf16[32,16,16,128]{3,2,1,0:T(8,128)(2,1)}, u32[]{:S(2)}, u32[]{:S(2)}) async-start(bf16[32,16,16,128]{3,2,1,0:T(8,128)(2,1)} %bitcast.11), calls=%async_computation | async-start | bytes 4194304 | tf_op jit(solution)/shard_map/all_to_all | solution.py:349
  81.6 110.0 %all-to-all-start.1 = ((bf16[128,4,16,128]{3,2,1,0:T(8,128)(2,1)}), bf16[128,4,16,128]{3,2,1,0:T(8,128)(2,1)}, u32[]{:S(2)}, u32[]{:S(2)}) async-start(bf16[128,4,16,128]{3,2,1,0:T(8,128)(2,1)} %bitcast.12), calls=%async_computation.1 | async-start | bytes 4194304 | tf_op jit(solution)/shard_map/all_to_all | solution.py:349
  105.0 51.6 %collective-permute-start = (bf16[4,128,1536]{2,1,0:T(8,128)(2,1)}, bf16[4,128,1536]{2,1,0:T(8,128)(2,1)S(1)}, u32[]{:S(2)}, u32[]{:S(2)}) collective-permute-start(bf16[4,128,1536]{2,1,0:T(8,128)(2,1)} %get-tuple-element.14), channel_id=1, source_target_pairs={{0,2},{2,4},{4,6},{6,0},{1,3},{3,5},{5,7},{7,1},{8,10},{10,12},{12... | collective-permute-start | bytes 4718600 | tf_op jit(solution)/shard_map/ppermute | solution.py:367
  106.5 85.1 %collective-permute-start.1 = (bf16[4,128,1536]{2,1,0:T(8,128)(2,1)}, bf16[4,128,1536]{2,1,0:T(8,128)(2,1)}, u32[]{:S(2)}, u32[]{:S(2)}) collective-permute-start(bf16[4,128,1536]{2,1,0:T(8,128)(2,1)} %get-tuple-element.15), channel_id=1, source_target_pairs={{0,4},{2,6},{4,0},{6,2},{1,5},{3,7},{5,1},{7,3},{8,12},{10,14},{12... | collective-permute-start | bytes 4718600 | tf_op jit(solution)/shard_map/ppermute | solution.py:367
  109.2 82.4 %collective-permute-start.2 = (bf16[4,128,1536]{2,1,0:T(8,128)(2,1)}, bf16[4,128,1536]{2,1,0:T(8,128)(2,1)}, u32[]{:S(2)}, u32[]{:S(2)}) collective-permute-start(bf16[4,128,1536]{2,1,0:T(8,128)(2,1)} %get-tuple-element.16), channel_id=1, source_target_pairs={{0,6},{2,0},{4,2},{6,4},{1,7},{3,1},{5,3},{7,5},{8,14},{10,8},{12,... | collective-permute-start | bytes 4718600 | tf_op jit(solution)/shard_map/ppermute | solution.py:367
  156.7 34.9 %copy-start = (bf16[4,128,1536]{2,1,0:T(8,128)(2,1)}, bf16[4,128,1536]{2,1,0:T(8,128)(2,1)S(1)}, u32[]{:S(2)}) copy-start(bf16[4,128,1536]{2,1,0:T(8,128)(2,1)S(1)} %collective-permute-done.rest_1_) | copy-start | bytes 4718596
where the time goes:
time: 245 us; the launch traced here: 244 us
  waiting for transfers between devices  128 us (52%)
  Pallas kernels  50.8 us (21%)
  blocking collectives  34 us (14%)
  starting transfers between devices  29.9 us (12%)
    ppermute x3, waiting for transfers between devices, on_device(): lax.ppermute(pieces[d], 'mem_y', [(i, (i + d) % parts) for i in range(par...  80.9 us
    all_to_all x2, waiting for transfers between devices, swap(): return lax.all_to_all(blocks, axes, 0, 0, tiled=True)  47.1 us
    all_to_all x2, blocking collectives, swap(): return lax.all_to_all(blocks, axes, 0, 0, tiled=True)  34 us
    all_to_all x2, starting transfers between devices, swap(): return lax.all_to_all(blocks, axes, 0, 0, tiled=True)  24.2 us
    pallas_call x1, Pallas kernels, backward(): pl.pallas_call(backward_kernel, grid_spec=pltpu.PrefetchScalarGridSpec(nu...  13 us
    pallas_call x1, Pallas kernels, forward(): pl.pallas_call(forward_kernel, grid=(members,), in_specs=[whole(modes.sha...  12.9 us
    pallas_call x1, Pallas kernels, divide(): pl.pallas_call(functools.partial(divide_kernel, rows=rows), grid_spec=plt...  10.8 us
    pallas_call x1, Pallas kernels, spectral(): pl.pallas_call(spectral_kernel, grid_spec=pltpu.PrefetchScalarGridSpec(nu...  8.59 us
  transfers between devices with their start and end apart: 5, of which 3 were waited for; matrix products, arithmetic and copies ran while one was open for 0% of the time, Pallas kernels for 4%

commit v1 on v0

v1 whole, which is shorter than its diff:
```python
import functools
import math

import jax
import jax.numpy as jnp
import numpy as np
from jax import lax
from jax.experimental import pallas as pl
from jax.experimental.pallas import tpu as pltpu
from jax.sharding import Mesh
from jax.sharding import PartitionSpec as P


NLON = 1536
M = 512
SPACE = ("space_0", "space_1", "space_2")
F32 = jnp.float32
BF16 = jnp.bfloat16
NT = (((1,), (1,)), ((), ()))
TN = (((0,), (0,)), ((), ()))


def angle_tables(block):
    points = np.arange(NLON)[None, :]
    amplitude = math.sqrt(2.0 / NLON)

    def angles(waves):
        return (points * waves[:, None] % NLON) * (2.0 * math.pi / NLON)

    low = angles(np.arange(block))
    high = angles(np.arange(M // block) * block)
    tables = (np.cos(low) * amplitude, np.sin(low) * amplitude, np.cos(high), np.sin(high))
    return [jnp.asarray(t, F32) for t in tables]


def iota2(shape, dim):
    return lax.broadcasted_iota(jnp.int32, shape, dim)


def over(value, size):
    assert size & (size - 1) == 0
    return value >> (size.bit_length() - 1)


def rest_of(value, size):
    assert size & (size - 1) == 0
    return value & (size - 1)


def one_hot(match):
    return jnp.where(match, 1.0, 0.0).astype(BF16)


def build_table(ft_ref, low_c, low_s, high_c, high_s):
    block = low_c.shape[0]

    def build(t, carry):
        hc = high_c[pl.ds(t, 1), :]
        hs = high_s[pl.ds(t, 1), :]
        at = pl.multiple_of(t * block, block)
        ft_ref[pl.ds(at, block), :] = (low_c[...] * hc - low_s[...] * hs).astype(BF16)
        ft_ref[pl.ds(M + at, block), :] = -(low_s[...] * hc + low_c[...] * hs).astype(BF16)
        return carry

    lax.fori_loop(0, M // block, build, 0)


def forward_kernel(modes_ref, low_c, low_s, high_c, high_s, e_hbm, v_hbm, z_hbm, ft, kp, p, y, e, v, z, arrive, leave):
    modes_n, levels = modes_ref.shape
    members = e.shape[0]
    rows = kp.shape[0] // modes_n
    fields = p.shape[0] // rows
    loads = [pltpu.make_async_copy(v_hbm, v, arrive.at[members])]
    for k in range(members):
        loads.append(pltpu.make_async_copy(e_hbm.at[k], e.at[k], arrive.at[k]))
    for load in loads:
        load.start()

    build_table(ft, low_c, low_s, high_c, high_s)
    ra = one_hot(rest_of(iota2((rows * modes_n, modes_n), 0), modes_n) == iota2((rows * modes_n, modes_n), 1))
    la = one_hot(over(iota2((levels, levels * rows), 1), rows) == iota2((levels, levels * rows), 0))
    spread_rows = jnp.dot(ra, modes_ref[...].astype(BF16), preferred_element_type=F32)
    full = jnp.dot(spread_rows.astype(BF16), la, preferred_element_type=F32)
    mask = over(iota2(kp.shape, 0), modes_n) == rest_of(iota2(kp.shape, 1), rows)
    kp[...] = jnp.where(mask, full, 0.0).astype(BF16)

    loads[0].wait()
    for k in range(members):
        loads[1 + k].wait()
        projected = jnp.dot(kp[...], e[k] * v[...], preferred_element_type=F32).astype(BF16)
        for a in range(rows):
            at = a * fields + k * modes_n
            p[at : at + modes_n, :] = projected[a * modes_n : (a + 1) * modes_n]

    lane = iota2((M, 2 * fields), 1)
    wide = 4 * fields
    for chunk in range(rows // 4):
        got = lax.dot_general(
            ft[...], p[chunk * wide : (chunk + 1) * wide, :], NT, preferred_element_type=F32
        )
        for pair in range(2):
            lanes = slice(pair * 2 * fields, (pair + 1) * 2 * fields)
            tc = got[:M, lanes]
            ts = got[M:, lanes]
            a = chunk * 4 + pair * 2
            y[pl.ds(a, M, stride=rows), :] = jnp.where(lane < fields, tc, pltpu.roll(ts, fields, 1))
            y[pl.ds(a + 1, M, stride=rows), :] = jnp.where(lane < fields, pltpu.roll(tc, fields, 1), ts)

    stores = []
    count = leave.shape[0]
    size = z.shape[0] // count
    for i in range(count):
        part = pl.ds(i * size, size)
        z[part, :] = y[part, :].astype(BF16)
        stores.append(pltpu.make_async_copy(z.at[part], z_hbm.at[part], leave.at[i]))
        stores[i].start()
    for store in stores:
        store.wait()


def forward(modes, ensemble, vector):
    members, levels, rows, lons = ensemble.shape
    modes_n = modes.shape[0]
    fields = members * modes_n
    tables = angle_tables(16)
    whole = pl.BlockSpec(memory_space=pltpu.MemorySpace.VMEM)
    outside = pl.BlockSpec(memory_space=pltpu.MemorySpace.HBM)
    return pl.pallas_call(
        forward_kernel,
        in_specs=[whole] * 5 + [outside] * 2,
        out_specs=outside,
        out_shape=jax.ShapeDtypeStruct((M * rows, 2 * fields), BF16),
        scratch_shapes=[
            pltpu.VMEM((2 * M, lons), BF16),
            pltpu.VMEM((rows * modes_n, levels * rows), BF16),
            pltpu.VMEM((rows * fields, lons), BF16),
            pltpu.VMEM((M * rows, 2 * fields), F32),
            pltpu.VMEM((members, levels * rows, lons), BF16),
            pltpu.VMEM((levels * rows, lons), BF16),
            pltpu.VMEM((M * rows, 2 * fields), BF16),
            pltpu.SemaphoreType.DMA((members + 1,)),
            pltpu.SemaphoreType.DMA((8,)),
        ],
        compiler_params=pltpu.CompilerParams(vmem_limit_bytes=62 * 2**20),
        name="forward",
    )(
        modes,
        *tables,
        ensemble.reshape(members, levels * rows, lons),
        vector.reshape(levels * rows, lons),
    )


def divide_kernel(scalars, modes_ref, low_c, low_s, high_c, high_s, e_ref, *rest, rows, halves):
    *out_refs, ft_ref, kl, order, perm = rest
    parts = len(out_refs)
    share = out_refs[0].shape[1]
    modes_n, levels = modes_ref.shape
    per = rows // parts
    columns = per * modes_n

    @pl.when(pl.program_id(0) == 0)
    def _():
        build_table(ft_ref, low_c, low_s, high_c, high_s)
        row = iota2(perm.shape, 0)
        col = iota2(perm.shape, 1)
        part = rest_of(scalars[2] + over(row, share), parts)
        level = over(rest_of(row, share), per)
        perm[...] = one_hot(col == level * rows + part * per + rest_of(row, per))
        level = over(row, rows)
        lat = rest_of(row, rows)
        half = levels // halves
        source = over(lat, per) * halves + over(level, half)
        order[...] = one_hot(col == source * (half * per) + rest_of(level, half) * per + rest_of(lat, per))
        height, width = kl.shape
        la = one_hot(over(rest_of(iota2((height, levels), 0), share), per) == iota2((height, levels), 1))
        ra = one_hot(rest_of(iota2((modes_n, width), 1), modes_n) == iota2((modes_n, width), 0))
        spread_rows = lax.dot_general(la, modes_ref[...].astype(BF16), NT, preferred_element_type=F32)
        full = jnp.dot(spread_rows.astype(BF16), ra, preferred_element_type=F32)
        row = iota2(kl.shape, 0)
        col = iota2(kl.shape, 1)
        mask = (over(row, share) == over(col, columns)) & (
            rest_of(row, per) == over(rest_of(col, columns), modes_n)
        )
        kl[...] = jnp.where(mask, full, 0.0).astype(BF16)

    moved = jnp.dot(perm[...], e_ref[0], preferred_element_type=F32).astype(BF16)
    for d, out_ref in enumerate(out_refs):
        out_ref[0] = moved[d * share : (d + 1) * share]


def divide(scalars, modes, ensemble, parts, halves):
    members, levels, rows, lons = ensemble.shape
    height = levels * rows
    share = height // parts
    columns = members * rows // parts * modes.shape[0]
    tables = angle_tables(16)
    fixed = lambda shape: pl.BlockSpec(shape, lambda k, _: (0, 0))
    return pl.pallas_call(
        functools.partial(divide_kernel, rows=rows, halves=halves),
        grid_spec=pltpu.PrefetchScalarGridSpec(
            num_scalar_prefetch=1,
            grid=(members,),
            in_specs=[fixed(t.shape) for t in (modes, *tables)]
            + [pl.BlockSpec((1, height, lons), lambda k, _: (k, 0, 0))],
            out_specs=[pl.BlockSpec((1, share, lons), lambda k, _: (k, 0, 0))] * parts
            + [fixed((2 * M, lons)), fixed((members * share, columns)), fixed((height, height))],
            scratch_shapes=[pltpu.VMEM((height, height), BF16)],
        ),
        out_shape=[jax.ShapeDtypeStruct((members, share, lons), BF16)] * parts
        + [
            jax.ShapeDtypeStruct((2 * M, lons), BF16),
            jax.ShapeDtypeStruct((members * share, columns), BF16),
            jax.ShapeDtypeStruct((height, height), BF16),
        ],
        compiler_params=pltpu.CompilerParams(vmem_limit_bytes=62 * 2**20),
        cost_estimate=pl.CostEstimate(flops=10**10, bytes_accessed=2 * 10**7, transcendentals=0),
        name="divide",
    )(scalars, modes, *tables, ensemble.reshape(members, height, lons))


def spectral_kernel(scalars, spectrum_ref, x_ref, l_hbm, out_ref, s, l_all, arrive):
    step = pl.program_id(0)
    sources, per, rows, lanes = x_ref.shape
    waves = l_all.shape[0]
    degrees = l_all.shape[2]

    def load(at):
        part = pl.ds(at * per, per)
        return pltpu.make_async_copy(l_hbm.at[part], l_all.at[part], arrive.at[at])

    @pl.when(step == 0)
    def _():
        for at in range(waves // per):
            load(at).start()

    load(step).wait()
    for i in range(per):
        m = step * per + i
        x = x_ref[:, i].reshape(sources * rows, lanes)
        harmonic = lax.dot_general(x, l_all[m], TN, preferred_element_type=F32)
        total = scalars[1] + m + iota2((1, degrees), 1)
        factor = jnp.where(total <= scalars[0], spectrum_ref[pl.ds(m, 1), :], 0.0)
        weighted = (harmonic * factor).astype(BF16)
        back = lax.dot_general(l_all[m], weighted, NT, preferred_element_type=F32)
        s[pl.ds(m, sources * rows, stride=waves), :] = back

    @pl.when(step == pl.num_programs(0) - 1)
    def _():
        out_ref[...] = s[...].astype(BF16)


def spectral(scalars, spectrum, arrived, legendre):
    sources, waves, rows, lanes = arrived.shape
    lats, degrees = legendre.shape[1:]
    per = 4
    return pl.pallas_call(
        spectral_kernel,
        grid_spec=pltpu.PrefetchScalarGridSpec(
            num_scalar_prefetch=1,
            grid=(waves // per,),
            in_specs=[
                pl.BlockSpec((waves, degrees), lambda i, _: (0, 0)),
                pl.BlockSpec((sources, per, rows, lanes), lambda i, _: (0, i, 0, 0)),
                pl.BlockSpec(memory_space=pltpu.MemorySpace.HBM),
            ],
            out_specs=pl.BlockSpec((sources * rows * waves, lanes), lambda i, _: (0, 0)),
            scratch_shapes=[
                pltpu.VMEM((sources * rows * waves, lanes), F32),
                pltpu.VMEM((waves, lats, degrees), BF16),
                pltpu.SemaphoreType.DMA((waves // per,)),
            ],
        ),
        out_shape=jax.ShapeDtypeStruct((sources * rows * waves, lanes), BF16),
        compiler_params=pltpu.CompilerParams(vmem_limit_bytes=50 * 2**20),
        name="spectral",
    )(scalars, spectrum, arrived, legendre)


def backward_kernel(scalars, kl_ref, r_ref, ft_ref, *rest):
    *e_refs, kept_ref, sent_ref, g, sums = rest
    sources, parts, rows, waves, lanes = r_ref.shape
    members, share = e_refs[0].shape[:2]
    fields = lanes // 2
    modes_n = fields // members
    columns = rows * modes_n

    @pl.when(pl.program_id(0) == 0)
    def _():
        for d in range(parts):
            source = rest_of(scalars[2] + parts - d, parts)
            for a in range(rows):
                flipped = r_ref[:, source, a].reshape(sources * waves, lanes).T
                for r in range(2):
                    for k in range(members):
                        at = r * fields + k * modes_n
                        to = (d * members + k) * columns + a * modes_n
                        g[to : to + modes_n, r * M : (r + 1) * M] = flipped[at : at + modes_n]

    spread = jnp.dot(g[...], ft_ref[...], preferred_element_type=F32).astype(BF16)
    group = members * columns
    total = None
    for d in range(parts):
        lifted = jnp.dot(kl_ref[...], spread[d * group : (d + 1) * group], preferred_element_type=F32)
        for k in range(members):
            term = e_refs[d][k].astype(F32) * lifted[k * share : (k + 1) * share]
            total = term if total is None else total + term
    sums[...] = total.astype(BF16)
    half = kept_ref.shape[0]
    at = scalars[3] * half
    kept_ref[...] = sums[pl.ds(pl.multiple_of(at, half), half), :]
    sent_ref[...] = sums[pl.ds(pl.multiple_of(half - at, half), half), :]


def backward(scalars, lift, returned, fourier, pieces, halves):
    _, parts, _, _, _ = returned.shape
    members, share, lons = pieces[0].shape
    chunk = 256
    half = share // halves
    return pl.pallas_call(
        backward_kernel,
        grid_spec=pltpu.PrefetchScalarGridSpec(
            num_scalar_prefetch=1,
            grid=(lons // chunk,),
            in_specs=[
                pl.BlockSpec(lift.shape, lambda i, _: (0, 0)),
                pl.BlockSpec(returned.shape, lambda i, _: (0, 0, 0, 0, 0)),
                pl.BlockSpec((2 * M, chunk), lambda i, _: (0, i)),
            ]
            + [pl.BlockSpec((members, share, chunk), lambda i, _: (0, 0, i))] * parts,
            out_specs=[pl.BlockSpec((half, chunk), lambda i, _: (0, i))] * halves,
            scratch_shapes=[
                pltpu.VMEM((parts * lift.shape[1], 2 * M), BF16),
                pltpu.VMEM((share, chunk), BF16),
            ],
        ),
        out_shape=[jax.ShapeDtypeStruct((half, lons), BF16)] * halves,
        compiler_params=pltpu.CompilerParams(vmem_limit_bytes=50 * 2**20),
        name="backward",
    )(scalars, lift, returned, fourier, *pieces)


def place_kernel(order_ref, x_ref, out_ref):
    out_ref[...] = jnp.dot(order_ref[...], x_ref[...], preferred_element_type=F32).astype(BF16)


def place(order, gathered):
    height, lons = gathered.shape
    chunk = 512
    return pl.pallas_call(
        place_kernel,
        grid=(lons // chunk,),
        in_specs=[
            pl.BlockSpec(order.shape, lambda i: (0, 0)),
            pl.BlockSpec((height, chunk), lambda i: (0, i)),
        ],
        out_specs=pl.BlockSpec((height, chunk), lambda i: (0, i)),
        out_shape=jax.ShapeDtypeStruct((height, lons), BF16),
        compiler_params=pltpu.CompilerParams(vmem_limit_bytes=16 * 2**20),
        name="place",
    )(order, gathered)


def swap(blocks, axes):
    return lax.all_to_all(blocks, axes, 0, 0, tiled=True)


def on_device(ensemble, vector, modes, legendre, spectrum, truncation):
    members, levels, rows, lons = ensemble.shape
    waves = legendre.shape[0]
    sources = lax.axis_size(SPACE)
    parts = lax.axis_size("mem_y")
    halves = lax.axis_size("mem_z")
    lanes = 2 * members * modes.shape[0]
    quarter = rows // parts
    first_wave = lax.axis_index(SPACE) * waves
    places = [first_wave, lax.axis_index("mem_y"), lax.axis_index("mem_z")]
    scalars = jnp.stack([truncation[0], *[i.astype(jnp.int32) for i in places]])
    zonal = forward(modes, ensemble, vector)
    arrived = swap(zonal.reshape(sources, waves, rows, lanes), SPACE)
    held, _ = lax.optimization_barrier((ensemble, zonal))
    *pieces, fourier, lift, order = divide(scalars, modes, held, parts, halves)
    for d in range(1, parts):
        pieces[d] = lax.ppermute(pieces[d], "mem_y", [(i, (i + d) % parts) for i in range(parts)])
    synthesis = spectral(scalars, spectrum, arrived, legendre)
    returned = swap(synthesis.reshape(sources * parts, quarter, waves, lanes), SPACE + ("mem_y",))
    returned = returned.reshape(sources, parts, quarter, waves, lanes)
    kept, sent = backward(scalars, lift, returned, fourier, pieces, halves)
    came = lax.ppermute(sent, "mem_z", [(0, 1), (1, 0)])
    share = kept.astype(F32) + came.astype(F32)
    rounded = (share / (members * parts * halves - 1)).astype(BF16)
    everyone = jnp.broadcast_to(rounded[None], (parts * halves, *rounded.shape))
    gathered = swap(everyone, ("mem_y", "mem_z"))
    return place(order, gathered.reshape(levels * rows, lons)).reshape(levels, rows, lons)


def solution(mesh):
    torus = Mesh(
        mesh.devices.reshape(4, 4, 2, 4, 2), ("space_0", "space_1", "space_2", "mem_y", "mem_z")
    )
    in_specs = (
        P(("mem_y", "mem_z"), None, SPACE, None),
        P(None, SPACE, None),
        P(),
        P(SPACE, None, None),
        P(SPACE, None),
        P(),
    )
    out_specs = P(None, SPACE, None)
    return jax.shard_map(on_device, mesh=torus, in_specs=in_specs, out_specs=out_specs, check_vma=False)
```

time: 245 us -> 241 us (0.984)
  blocking collectives: 34 us -> 25.6 us
  starting transfers between devices: 29.9 us -> 37.2 us
  Pallas kernels: 50.8 us -> 45.2 us
    all_to_all x2 -> x1, blocking collectives: 34 us -> 25.6 us  [swap(): return lax.all_to_all(blocks, axes, 0, 0, tiled=True)]
    ppermute x0 -> x1, starting transfers between devices: none -> 7.15 us  [on_device(): came = lax.ppermute(sent, 'mem_z', [(0, 1), (1, 0)])]
    pallas_call x3, Pallas kernels: 29.3 us -> 24.7 us  [the longest x1 11.5 us: divide(): pl.pallas_call(functools.partial(divide_kernel, rows=rows, halves=halves)...]
    ppermute x0 -> x1, waiting for transfers between devices: none -> 4.12 us  [on_device(): came = lax.ppermute(sent, 'mem_z', [(0, 1), (1, 0)])]
    ppermute x3, waiting for transfers between devices: 80.9 us -> 77.6 us  [on_device(): lax.ppermute(pieces[d], 'mem_y', [(i, (i + d) % parts) for i in range(par...]
  transfers between devices with their start and end apart: 5 -> 6, of which waited for: 3 -> 4; matrix products, arithmetic and copies ran while one was open for 0% -> 0% of each run, Pallas kernels for 4% -> 5%
where the time goes in v1:
time: 241 us; the launch traced here: 240 us
  waiting for transfers between devices  128 us (53%)
  Pallas kernels  45.2 us (19%)
  starting transfers between devices  37.2 us (15%)
  blocking collectives  25.6 us (11%)
  local copies, waits for them, and re-layouts  2.49 us (1%)
    ppermute x3, waiting for transfers between devices, on_device(): lax.ppermute(pieces[d], 'mem_y', [(i, (i + d) % parts) for i in range(par...  77.6 us
    all_to_all x2, waiting for transfers between devices, swap(): return lax.all_to_all(blocks, axes, 0, 0, tiled=True)  46.7 us
    all_to_all x1, blocking collectives, swap(): return lax.all_to_all(blocks, axes, 0, 0, tiled=True)  25.6 us
    all_to_all x2, starting transfers between devices, swap(): return lax.all_to_all(blocks, axes, 0, 0, tiled=True)  24.4 us
    pallas_call x1, Pallas kernels, backward(): pl.pallas_call(backward_kernel, grid_spec=pltpu.PrefetchScalarGridSpec(nu...  12 us
    pallas_call x1, Pallas kernels, divide(): pl.pallas_call(functools.partial(divide_kernel, rows=rows, halves=halves)...  11.5 us
    pallas_call x1, Pallas kernels, forward(): pl.pallas_call(forward_kernel, in_specs=[whole] * 5 + [outside] * 2, out_...  10.6 us
    pallas_call x1, Pallas kernels, spectral(): pl.pallas_call(spectral_kernel, grid_spec=pltpu.PrefetchScalarGridSpec(nu...  8.45 us
  transfers between devices with their start and end apart: 6, of which 4 were waited for; matrix products, arithmetic and copies ran while one was open for 0% of the time, Pallas kernels for 5%

profile of v1, /device:TPU:2, one launch (start us, length us, event | category | flops | bytes accessed | tf_op | source)
XLA Modules:
  0.0 239.8 jit_solution(10302469177745374598)
XLA Ops:
  0.0 10.6 %forward.1 = bf16[8192,128]{1,0:T(8,128)(2,1)} custom-call(f32[16,32]{1,0:T(8,128)} %modes_ref.3, f32[16,1536]{1,0:T(8,128)} %constant.36.clone.low_c, f32[16,1536]{1,0:T(8,128)} %constant.37.clone.low_s, f32[32,1536]{1,0:T(8,128)} %constant.38.clone.high_c, f32[32,1536]{1,0:T(8,128)} %constant.39.clone.high_s, bf16[4,512,1536]{2,1,0:T(8,128)(2,1)} %bitcast.13, ...), custom_call_target="tpu_custom_call" | custom-call | tf_op jit(solution)/shard_map/forward/pallas_call | solution.py:128
  10.6 0.0 copy-start.3
  10.7 11.7 %all-to-all-start = ((bf16[32,16,16,128]{3,2,1,0:T(8,128)(2,1)}), bf16[32,16,16,128]{3,2,1,0:T(8,128)(2,1)}, u32[]{:S(2)}, u32[]{:S(2)}) async-start(bf16[32,16,16,128]{3,2,1,0:T(8,128)(2,1)} %bitcast.12), calls=%async_computation | async-start | bytes 4194304 | tf_op jit(solution)/shard_map/all_to_all | solution.py:365
  23.0 0.1 pad_add_fusion.scalars
  23.1 46.7 %all-to-all-done.x_ref = bf16[32,16,16,128]{3,2,1,0:T(8,128)(2,1)} async-done(((bf16[32,16,16,128]{3,2,1,0:T(8,128)(2,1)}), bf16[32,16,16,128]{3,2,1,0:T(8,128)(2,1)}, u32[]{:S(2)}, u32[]{:S(2)}) %all-to-all-start) | async-done | bytes 2097184 | tf_op jit(solution)/shard_map/all_to_all | solution.py:365
  69.8 8.4 %spectral.1 = bf16[8192,128]{1,0:T(8,128)(2,1)} custom-call(s32[4]{0:T(128)S(1)} %pad_add_fusion.scalars, f32[16,256]{1,0:T(8,128)S(1)} %copy-done.3, bf16[32,16,16,128]{3,2,1,0:T(8,128)(2,1)} %all-to-all-done.x_ref, bf16[16,512,256]{2,1,0:T(8,128)(2,1)} %l_hbm.1), custom_call_target="tpu_custom_call" | custom-call | tf_op jit(solution)/shard_map/spectral/pallas_call | solution.py:257
  78.3 12.8 %all-to-all-start.1 = ((bf16[128,4,16,128]{3,2,1,0:T(8,128)(2,1)}), bf16[128,4,16,128]{3,2,1,0:T(8,128)(2,1)}, u32[]{:S(2)}, u32[]{:S(2)}) async-start(bf16[128,4,16,128]{3,2,1,0:T(8,128)(2,1)} %bitcast.7), calls=%async_computation.1 | async-start | bytes 4194304 | tf_op jit(solution)/shard_map/all_to_all | solution.py:365
  91.1 11.5 %divide.1 = (bf16[4,128,1536]{2,1,0:T(8,128)(2,1)}, bf16[4,128,1536]{2,1,0:T(8,128)(2,1)}, bf16[4,128,1536]{2,1,0:T(8,128)(2,1)}, bf16[4,128,1536]{2,1,0:T(8,128...) custom-call(s32[4]{0:T(128)} %copy-done.4, f32[16,32]{1,0:T(8,128)} %modes_ref.3, ...), custom_call_target="tpu_custom_call" | custom-call | flops 10000000000 | bytes 20000000 | tf_op jit(solution)/shard_map/divide/pallas_call | solution.py:199
  102.6 1.5 collective-permute-start
  104.1 2.7 %collective-permute-start.1 = (bf16[4,128,1536]{2,1,0:T(8,128)(2,1)}, bf16[4,128,1536]{2,1,0:T(8,128)(2,1)}, u32[]{:S(2)}, u32[]{:S(2)}) collective-permute-start(bf16[4,128,1536]{2,1,0:T(8,128)(2,1)} %get-tuple-element.21), channel_id=1, source_target_pairs={{0,4},{2,6},{4,0},{6,2},{1,5},{3,7},{5,1},{7,3},{8,12},{10,14},{12... | collective-permute-start | bytes 4718600 | tf_op jit(solution)/shard_map/ppermute | solution.py:384
  106.8 1.5 collective-permute-start.2
  108.2 43.0 %collective-permute-done.rest_1_ = bf16[4,128,1536]{2,1,0:T(8,128)(2,1)S(1)} collective-permute-done((bf16[4,128,1536]{2,1,0:T(8,128)(2,1)}, bf16[4,128,1536]{2,1,0:T(8,128)(2,1)S(1)}, u32[]{:S(2)}, u32[]{:S(2)}) %collective-permute-start) | collective-permute-done | bytes 1572896 | tf_op jit(solution)/shard_map/ppermute | solution.py:384
  151.2 34.6 %collective-permute-done.1.rest_2_ = bf16[4,128,1536]{2,1,0:T(8,128)(2,1)} collective-permute-done((bf16[4,128,1536]{2,1,0:T(8,128)(2,1)}, bf16[4,128,1536]{2,1,0:T(8,128)(2,1)}, u32[]{:S(2)}, u32[]{:S(2)}) %collective-permute-start.1) | collective-permute-done | bytes 1572896 | tf_op jit(solution)/shard_map/ppermute | solution.py:384
  185.8 0.0 collective-permute-done.2.rest_3_
  185.8 0.0 copy-start
  185.8 1.4 copy-done
  187.2 0.9 copy-done.2
  188.2 12.0 %backward.1 = (bf16[64,1536]{1,0:T(8,128)(2,1)S(1)}, bf16[64,1536]{1,0:T(8,128)(2,1)S(1)}) custom-call(s32[4]{0:T(128)S(1)} %copy-done.5, bf16[512,256]{1,0:T(8,128)(2,1)S(1)} %copy-done.2, bf16[32,4,4,16,128]{4,3,2,1,0:T(8,128)(2,1)} %bitcast.8.r_ref, bf16[1024,1536]{1,0:T(8,128)(2,1)} %get-tuple-element.18.ft_ref, bf16[4,128,1536]{2,1,0:T(8,128)(2,1)S(1)} %copy-done, ...), custom_call_target="tpu_custom_call" | custom-call | tf_op jit(solution)/shard_map/backward/pallas_call | solution.py:320
  200.2 7.1 %collective-permute-start.3 = (bf16[64,1536]{1,0:T(8,128)(2,1)S(1)}, bf16[64,1536]{1,0:T(8,128)(2,1)S(1)}, u32[]{:S(2)}, u32[]{:S(2)}) collective-permute-start(bf16[64,1536]{1,0:T(8,128)(2,1)S(1)} %get-tuple-element.24), channel_id=1, source_target_pairs={{0,1},{1,0},{2,3},{3,2},{4,5},{5,4},{6,7},{7,6},{8,9},{9,8},{10,11... | collective-permute-start | bytes 589832 | tf_op jit(solution)/shard_map/ppermute | solution.py:389
  207.4 4.1 %collective-permute-done.3 = bf16[64,1536]{1,0:T(8,128)(2,1)S(1)} collective-permute-done((bf16[64,1536]{1,0:T(8,128)(2,1)S(1)}, bf16[64,1536]{1,0:T(8,128)(2,1)S(1)}, u32[]{:S(2)}, u32[]{:S(2)}) %collective-permute-start.3) | collective-permute-done | bytes 196640 | tf_op jit(solution)/shard_map/ppermute | solution.py:389
  211.5 0.1 multiply_convert_fusion
  211.6 0.1 broadcast_in_dim.2
  211.7 25.6 %all_to_all.15 = bf16[8,64,1536]{2,1,0:T(8,128)(2,1)S(1)} all-to-all(bf16[8,64,1536]{2,1,0:T(8,128)(2,1)S(1)} %broadcast_in_dim.2), channel_id=1, replica_groups=mesh['space_0'=4,'space_1'=4,'space_2'=2,'mem_y'=4,'mem_z'=2] {'mem_y','..., dimensions={0} | all-to-all | bytes 3145728 | tf_op jit(solution)/shard_map/all_to_all | solution.py:365
  237.3 2.6 %place.1 = bf16[512,1536]{1,0:T(8,128)(2,1)} custom-call(bf16[512,512]{1,0:T(8,128)(2,1)S(1)} %copy-done.1, bf16[512,1536]{1,0:T(8,128)(2,1)S(1)} %bitcast.11), custom_call_target="tpu_custom_call" | custom-call | tf_op jit(solution)/shard_map/place/pallas_call | solution.py:350
  (9 shorter events, 0.0 us)
Async XLA Ops:
  10.6 59.1 %copy-start.3 = (f32[16,256]{1,0:T(8,128)S(1)}, f32[16,256]{1,0:T(8,128)}, u32[]{:S(2)}) copy-start(f32[16,256]{1,0:T(8,128)} %spectrum_ref.1) | copy-start | bytes 49156
  10.7 59.1 %all-to-all-start = ((bf16[32,16,16,128]{3,2,1,0:T(8,128)(2,1)}), bf16[32,16,16,128]{3,2,1,0:T(8,128)(2,1)}, u32[]{:S(2)}, u32[]{:S(2)}) async-start(bf16[32,16,16,128]{3,2,1,0:T(8,128)(2,1)} %bitcast.12), calls=%async_computation | async-start | bytes 4194304 | tf_op jit(solution)/shard_map/all_to_all | solution.py:365
  23.1 55.2 %copy-start.4 = (s32[4]{0:T(128)}, s32[4]{0:T(128)S(1)}, u32[]{:S(2)}) copy-start(s32[4]{0:T(128)S(1)} %pad_add_fusion.scalars) | copy-start | bytes 52
  78.3 107.6 %all-to-all-start.1 = ((bf16[128,4,16,128]{3,2,1,0:T(8,128)(2,1)}), bf16[128,4,16,128]{3,2,1,0:T(8,128)(2,1)}, u32[]{:S(2)}, u32[]{:S(2)}) async-start(bf16[128,4,16,128]{3,2,1,0:T(8,128)(2,1)} %bitcast.7), calls=%async_computation.1 | async-start | bytes 4194304 | tf_op jit(solution)/shard_map/all_to_all | solution.py:365
  91.0 94.8 %copy-start.5 = (s32[4]{0:T(128)S(1)}, s32[4]{0:T(128)}, u32[]{:S(2)}) copy-start(s32[4]{0:T(128)} %copy-done.4) | copy-start | bytes 52
  102.6 48.6 %collective-permute-start = (bf16[4,128,1536]{2,1,0:T(8,128)(2,1)}, bf16[4,128,1536]{2,1,0:T(8,128)(2,1)S(1)}, u32[]{:S(2)}, u32[]{:S(2)}) collective-permute-start(bf16[4,128,1536]{2,1,0:T(8,128)(2,1)} %get-tuple-element.20), channel_id=1, source_target_pairs={{0,2},{2,4},{4,6},{6,0},{1,3},{3,5},{5,7},{7,1},{8,10},{10,12},{12... | collective-permute-start | bytes 4718600 | tf_op jit(solution)/shard_map/ppermute | solution.py:384
  104.1 81.7 %collective-permute-start.1 = (bf16[4,128,1536]{2,1,0:T(8,128)(2,1)}, bf16[4,128,1536]{2,1,0:T(8,128)(2,1)}, u32[]{:S(2)}, u32[]{:S(2)}) collective-permute-start(bf16[4,128,1536]{2,1,0:T(8,128)(2,1)} %get-tuple-element.21), channel_id=1, source_target_pairs={{0,4},{2,6},{4,0},{6,2},{1,5},{3,7},{5,1},{7,3},{8,12},{10,14},{12... | collective-permute-start | bytes 4718600 | tf_op jit(solution)/shard_map/ppermute | solution.py:384
  106.8 79.1 %collective-permute-start.2 = (bf16[4,128,1536]{2,1,0:T(8,128)(2,1)}, bf16[4,128,1536]{2,1,0:T(8,128)(2,1)}, u32[]{:S(2)}, u32[]{:S(2)}) collective-permute-start(bf16[4,128,1536]{2,1,0:T(8,128)(2,1)} %get-tuple-element.22), channel_id=1, source_target_pairs={{0,6},{2,0},{4,2},{6,4},{1,7},{3,1},{5,3},{7,5},{8,14},{10,8},{12,... | collective-permute-start | bytes 4718600 | tf_op jit(solution)/shard_map/ppermute | solution.py:384
  185.8 1.4 copy-start
  187.2 0.9 copy-start.2
  200.2 11.3 %collective-permute-start.3 = (bf16[64,1536]{1,0:T(8,128)(2,1)S(1)}, bf16[64,1536]{1,0:T(8,128)(2,1)S(1)}, u32[]{:S(2)}, u32[]{:S(2)}) collective-permute-start(bf16[64,1536]{1,0:T(8,128)(2,1)S(1)} %get-tuple-element.24), channel_id=1, source_target_pairs={{0,1},{1,0},{2,3},{3,2},{4,5},{5,4},{6,7},{7,6},{8,9},{9,8},{10,11... | collective-permute-start | bytes 589832 | tf_op jit(solution)/shard_map/ppermute | solution.py:389
  211.7 25.6 %copy-start.1 = (bf16[512,512]{1,0:T(8,128)(2,1)S(1)}, bf16[512,512]{1,0:T(8,128)(2,1)}, u32[]{:S(2)}) copy-start(bf16[512,512]{1,0:T(8,128)(2,1)} %get-tuple-element.16.order_ref) | copy-start | bytes 1572868

commit v2 on v1

--- a/solution.py
+++ b/solution.py
@@ -151,127 +151,153 @@
     )
 
 
-def divide_kernel(scalars, modes_ref, low_c, low_s, high_c, high_s, e_ref, *rest, rows, halves):
-    *out_refs, ft_ref, kl, order, perm = rest
+def divide_kernel(scalars, e_ref, *rest, rows):
+    *out_refs, perm = rest
     parts = len(out_refs)
     share = out_refs[0].shape[1]
+    per = rows // parts
+
+    @pl.when(pl.program_id(0) == 0)
+    def _():
+        row = iota2(perm.shape, 0)
+        part = rest_of(scalars[2] + over(row, share), parts)
+        level = over(rest_of(row, share), per)
+        perm[...] = one_hot(iota2(perm.shape, 1) == level * rows + part * per + rest_of(row, per))
+
+    moved = jnp.dot(perm[...], e_ref[0], preferred_element_type=F32).astype(BF16)
+    for d, out_ref in enumerate(out_refs):
+        out_ref[0] = moved[d * share : (d + 1) * share]
+
+
+def divide(scalars, ensemble, parts):
+    members, levels, rows, lons = ensemble.shape
+    height = levels * rows
+    share = height // parts
+    return pl.pallas_call(
+        functools.partial(divide_kernel, rows=rows),
+        grid_spec=pltpu.PrefetchScalarGridSpec(
+            num_scalar_prefetch=1,
+            grid=(members,),
+            in_specs=[pl.BlockSpec((1, height, lons), lambda k, _: (k, 0, 0))],
+            out_specs=[pl.BlockSpec((1, share, lons), lambda k, _: (k, 0, 0))] * parts,
+            scratch_shapes=[pltpu.VMEM((height, height), BF16)],
+        ),
+        out_shape=[jax.ShapeDtypeStruct((members, share, lons), BF16)] * parts,
+        compiler_params=pltpu.CompilerParams(vmem_limit_bytes=62 * 2**20),
+        cost_estimate=pl.CostEstimate(flops=10**10, bytes_accessed=2 * 10**7, transcendentals=0),
+        name="divide",
+    )(scalars, ensemble.reshape(members, height, lons))
+
+
+def matrices_kernel(modes_ref, low_c, low_s, high_c, high_s, ft_ref, kl, order, *, rows, parts, halves):
     modes_n, levels = modes_ref.shape
     per = rows // parts
     columns = per * modes_n
-
-    @pl.when(pl.program_id(0) == 0)
-    def _():
-        build_table(ft_ref, low_c, low_s, high_c, high_s)
-        row = iota2(perm.shape, 0)
-        col = iota2(perm.shape, 1)
-        part = rest_of(scalars[2] + over(row, share), parts)
-        level = over(rest_of(row, share), per)
-        perm[...] = one_hot(col == level * rows + part * per + rest_of(row, per))
-        level = over(row, rows)
-        lat = rest_of(row, rows)
-        half = levels // halves
-        source = over(lat, per) * halves + over(level, half)
-        order[...] = one_hot(col == source * (half * per) + rest_of(level, half) * per + rest_of(lat, per))
-        height, width = kl.shape
-        la = one_hot(over(rest_of(iota2((height, levels), 0), share), per) == iota2((height, levels), 1))
-        ra = one_hot(rest_of(iota2((modes_n, width), 1), modes_n) == iota2((modes_n, width), 0))
-        spread_rows = lax.dot_general(la, modes_ref[...].astype(BF16), NT, preferred_element_type=F32)
-        full = jnp.dot(spread_rows.astype(BF16), ra, preferred_element_type=F32)
-        row = iota2(kl.shape, 0)
-        col = iota2(kl.shape, 1)
-        mask = (over(row, share) == over(col, columns)) & (
-            rest_of(row, per) == over(rest_of(col, columns), modes_n)
-        )
-        kl[...] = jnp.where(mask, full, 0.0).astype(BF16)
-
-    moved = jnp.dot(perm[...], e_ref[0], preferred_element_type=F32).astype(BF16)
-    for d, out_ref in enumerate(out_refs):
-        out_ref[0] = moved[d * share : (d + 1) * share]
-
-
-def divide(scalars, modes, ensemble, parts, halves):
-    members, levels, rows, lons = ensemble.shape
-    height = levels * rows
-    share = height // parts
-    columns = members * rows // parts * modes.shape[0]
+    share = levels * per
+    build_table(ft_ref, low_c, low_s, high_c, high_s)
+    row = iota2(order.shape, 0)
+    level = over(row, rows)
+    lat = rest_of(row, rows)
+    half = levels // halves
+    source = over(lat, per) * halves + over(level, half)
+    wanted = source * (half * per) + rest_of(level, half) * per + rest_of(lat, per)
+    order[...] = one_hot(iota2(order.shape, 1) == wanted)
+    height, width = kl.shape
+    la = one_hot(over(rest_of(iota2((height, levels), 0), share), per) == iota2((height, levels), 1))
+    ra = one_hot(rest_of(iota2((modes_n, width), 1), modes_n) == iota2((modes_n, width), 0))
+    spread_rows = lax.dot_general(la, modes_ref[...].astype(BF16), NT, preferred_element_type=F32)
+    full = jnp.dot(spread_rows.astype(BF16), ra, preferred_element_type=F32)
+    row = iota2(kl.shape, 0)
+    col = iota2(kl.shape, 1)
+    mask = (over(row, share) == over(col, columns)) & (
+        rest_of(row, per) == over(rest_of(col, columns), modes_n)
+    )
+    kl[...] = jnp.where(mask, full, 0.0).astype(BF16)
+
+
+def matrices(modes, members, rows, parts, halves):
+    modes_n, levels = modes.shape
+    per = rows // parts
     tables = angle_tables(16)
-    fixed = lambda shape: pl.BlockSpec(shape, lambda k, _: (0, 0))
-    return pl.pallas_call(
-        functools.partial(divide_kernel, rows=rows, halves=halves),
-        grid_spec=pltpu.PrefetchScalarGridSpec(
-            num_scalar_prefetch=1,
-            grid=(members,),
-            in_specs=[fixed(t.shape) for t in (modes, *tables)]
-            + [pl.BlockSpec((1, height, lons), lambda k, _: (k, 0, 0))],
-            out_specs=[pl.BlockSpec((1, share, lons), lambda k, _: (k, 0, 0))] * parts
-            + [fixed((2 * M, lons)), fixed((members * share, columns)), fixed((height, height))],
-            scratch_shapes=[pltpu.VMEM((height, height), BF16)],
-        ),
-        out_shape=[jax.ShapeDtypeStruct((members, share, lons), BF16)] * parts
-        + [
-            jax.ShapeDtypeStruct((2 * M, lons), BF16),
-            jax.ShapeDtypeStruct((members * share, columns), BF16),
-            jax.ShapeDtypeStruct((height, height), BF16),
+    whole = pl.BlockSpec(memory_space=pltpu.MemorySpace.VMEM)
+    return pl.pallas_call(
+        functools.partial(matrices_kernel, rows=rows, parts=parts, halves=halves),
+        in_specs=[whole] * 5,
+        out_specs=[whole] * 3,
+        out_shape=[
+            jax.ShapeDtypeStruct((2 * M, NLON), BF16),
+            jax.ShapeDtypeStruct((members * levels * per, members * per * modes_n), BF16),
+            jax.ShapeDtypeStruct((levels * rows, levels * rows), BF16),
         ],
         compiler_params=pltpu.CompilerParams(vmem_limit_bytes=62 * 2**20),
-        cost_estimate=pl.CostEstimate(flops=10**10, bytes_accessed=2 * 10**7, transcendentals=0),
-        name="divide",
-    )(scalars, modes, *tables, ensemble.reshape(members, height, lons))
-
-
-def spectral_kernel(scalars, spectrum_ref, x_ref, l_hbm, out_ref, s, l_all, arrive):
-    step = pl.program_id(0)
-    sources, per, rows, lanes = x_ref.shape
-    waves = l_all.shape[0]
-    degrees = l_all.shape[2]
-
-    def load(at):
-        part = pl.ds(at * per, per)
-        return pltpu.make_async_copy(l_hbm.at[part], l_all.at[part], arrive.at[at])
-
-    @pl.when(step == 0)
-    def _():
-        for at in range(waves // per):
-            load(at).start()
-
-    load(step).wait()
-    for i in range(per):
-        m = step * per + i
-        x = x_ref[:, i].reshape(sources * rows, lanes)
-        harmonic = lax.dot_general(x, l_all[m], TN, preferred_element_type=F32)
-        total = scalars[1] + m + iota2((1, degrees), 1)
-        factor = jnp.where(total <= scalars[0], spectrum_ref[pl.ds(m, 1), :], 0.0)
-        weighted = (harmonic * factor).astype(BF16)
-        back = lax.dot_general(l_all[m], weighted, NT, preferred_element_type=F32)
-        s[pl.ds(m, sources * rows, stride=waves), :] = back
-
-    @pl.when(step == pl.num_programs(0) - 1)
-    def _():
-        out_ref[...] = s[...].astype(BF16)
+        cost_estimate=pl.CostEstimate(flops=10**9, bytes_accessed=4 * 10**6, transcendentals=0),
+        name="matrices",
+    )(modes, *tables)
+
+
+def spectral_kernel(scalars, spectrum_ref, x_hbm, l_hbm, out_hbm, s, x, l, z, arrive_x, arrive_l, leave):
+    sources, waves, rows, lanes = x.shape
+    degrees = l.shape[2]
+    height = sources * rows
+    groups = arrive_x.shape[0]
+    per = waves // groups
+    loads = []
+    for i in range(groups):
+        part = pl.ds(i * per, per)
+        loads.append(
+            (
+                pltpu.make_async_copy(x_hbm.at[:, part], x.at[:, part], arrive_x.at[i]),
+                pltpu.make_async_copy(l_hbm.at[part], l.at[part], arrive_l.at[i]),
+            )
+        )
+        for load in loads[i]:
+            load.start()
+    for i in range(groups):
+        for load in loads[i]:
+            load.wait()
+        for m in range(i * per, (i + 1) * per):
+            own = x[:, m].reshape(height, lanes)
+            harmonic = lax.dot_general(own, l[m], TN, preferred_element_type=F32)
+            total = scalars[1] + m + iota2((1, degrees), 1)
+            factor = jnp.where(total <= scalars[0], spectrum_ref[m : m + 1, :], 0.0)
+            weighted = (harmonic * factor).astype(BF16)
+            back = lax.dot_general(l[m], weighted, NT, preferred_element_type=F32)
+            s[pl.ds(m, height, stride=waves), :] = back
+    stores = []
+    count = leave.shape[0]
+    size = height * waves // count
+    for i in range(count):
+        part = pl.ds(i * size, size)
+        z[part, :] = s[part, :].astype(BF16)
+        stores.append(pltpu.make_async_copy(z.at[part], out_hbm.at[part], leave.at[i]))
+        stores[i].start()
+    for store in stores:
+        store.wait()
 
 
 def spectral(scalars, spectrum, arrived, legendre):
     sources, waves, rows, lanes = arrived.shape
-    lats, degrees = legendre.shape[1:]
-    per = 4
+    height = sources * rows * waves
+    outside = pl.BlockSpec(memory_space=pltpu.MemorySpace.HBM)
     return pl.pallas_call(
         spectral_kernel,
-        grid_spec=pltpu.PrefetchScalarGridSpec(
-            num_scalar_prefetch=1,
-            grid=(waves // per,),
-            in_specs=[
-                pl.BlockSpec((waves, degrees), lambda i, _: (0, 0)),
-                pl.BlockSpec((sources, per, rows, lanes), lambda i, _: (0, i, 0, 0)),
-                pl.BlockSpec(memory_space=pltpu.MemorySpace.HBM),
-            ],
-            out_specs=pl.BlockSpec((sources * rows * waves, lanes), lambda i, _: (0, 0)),
-            scratch_shapes=[
-                pltpu.VMEM((sources * rows * waves, lanes), F32),
-                pltpu.VMEM((waves, lats, degrees), BF16),
-                pltpu.SemaphoreType.DMA((waves // per,)),
-            ],
-        ),
-        out_shape=jax.ShapeDtypeStruct((sources * rows * waves, lanes), BF16),
+        in_specs=[
+            pl.BlockSpec(memory_space=pltpu.MemorySpace.SMEM),
+            pl.BlockSpec(memory_space=pltpu.MemorySpace.VMEM),
+            outside,
+            outside,
+        ],
+        out_specs=outside,
+        out_shape=jax.ShapeDtypeStruct((height, lanes), BF16),
+        scratch_shapes=[
+            pltpu.VMEM((height, lanes), F32),
+            pltpu.VMEM(arrived.shape, BF16),
+            pltpu.VMEM(legendre.shape, BF16),
+            pltpu.VMEM((height, lanes), BF16),
+            pltpu.SemaphoreType.DMA((4,)),
+            pltpu.SemaphoreType.DMA((4,)),
+            pltpu.SemaphoreType.DMA((8,)),
+        ],
         compiler_params=pltpu.CompilerParams(vmem_limit_bytes=50 * 2**20),
         name="spectral",
     )(scalars, spectrum, arrived, legendre)
@@ -315,7 +341,7 @@
 def backward(scalars, lift, returned, fourier, pieces, halves):
     _, parts, _, _, _ = returned.shape
     members, share, lons = pieces[0].shape
-    chunk = 256
+    chunk = 512
     half = share // halves
     return pl.pallas_call(
         backward_kernel,
@@ -379,9 +405,10 @@
     zonal = forward(modes, ensemble, vector)
     arrived = swap(zonal.reshape(sources, waves, rows, lanes), SPACE)
     held, _ = lax.optimization_barrier((ensemble, zonal))
-    *pieces, fourier, lift, order = divide(scalars, modes, held, parts, halves)
+    pieces = list(divide(scalars, held, parts))
     for d in range(1, parts):
         pieces[d] = lax.ppermute(pieces[d], "mem_y", [(i, (i + d) % parts) for i in range(parts)])
+    fourier, lift, order = matrices(modes, members, rows, parts, halves)
     synthesis = spectral(scalars, spectrum, arrived, legendre)
     returned = swap(synthesis.reshape(sources * parts, quarter, waves, lanes), SPACE + ("mem_y",))
     returned = returned.reshape(sources, parts, quarter, waves, lanes)

time: 241 us -> 234 us (0.971)
  Pallas kernels: 45.2 us -> 42.4 us
    pallas_call x1, Pallas kernels: 12 us -> 9.21 us  [backward(): pl.pallas_call(backward_kernel, grid_spec=pltpu.PrefetchScalarGridSpec(nu...]
    pallas_call x2 -> x3, Pallas kernels: 20 us -> 19.9 us  [the longest x1 8.39 us: divide(): pl.pallas_call(functools.partial(divide_kernel, rows=rows), grid_spec=plt...]
where the time goes in v2:
time: 234 us; the launch traced here: 233 us
  waiting for transfers between devices  127 us (54%)
  Pallas kernels  42.4 us (18%)
  starting transfers between devices  35.4 us (15%)
  blocking collectives  25.5 us (11%)
  local copies, waits for them, and re-layouts  2.43 us (1%)
    ppermute x3, waiting for transfers between devices, on_device(): lax.ppermute(pieces[d], 'mem_y', [(i, (i + d) % parts) for i in range(par...  75.5 us
    all_to_all x2, waiting for transfers between devices, swap(): return lax.all_to_all(blocks, axes, 0, 0, tiled=True)  46.7 us
    all_to_all x1, blocking collectives, swap(): return lax.all_to_all(blocks, axes, 0, 0, tiled=True)  25.5 us
    all_to_all x2, starting transfers between devices, swap(): return lax.all_to_all(blocks, axes, 0, 0, tiled=True)  24.4 us
    pallas_call x1, Pallas kernels, forward(): pl.pallas_call(forward_kernel, in_specs=[whole] * 5 + [outside] * 2, out_...  10.7 us
    pallas_call x1, Pallas kernels, backward(): pl.pallas_call(backward_kernel, grid_spec=pltpu.PrefetchScalarGridSpec(nu...  9.21 us
    pallas_call x1, Pallas kernels, divide(): pl.pallas_call(functools.partial(divide_kernel, rows=rows), grid_spec=plt...  8.39 us
    pallas_call x1, Pallas kernels, spectral(): pl.pallas_call(spectral_kernel, in_specs=[pl.BlockSpec(memory_space=pltpu...  7.23 us
  transfers between devices with their start and end apart: 6, of which 4 were waited for; matrix products, arithmetic and copies ran while one was open for 0% of the time, Pallas kernels for 5%

profile of v2, /device:TPU:2, one launch (start us, length us, event | category | flops | bytes accessed | tf_op | source)
XLA Modules:
  0.0 233.3 jit_solution(18416516943570397609)
XLA Ops:
  0.0 10.7 %forward.1 = bf16[8192,128]{1,0:T(8,128)(2,1)} custom-call(f32[16,32]{1,0:T(8,128)} %modes_ref.3, f32[16,1536]{1,0:T(8,128)} %constant.36.clone.low_c, f32[16,1536]{1,0:T(8,128)} %constant.37.clone.low_s, f32[32,1536]{1,0:T(8,128)} %constant.38.clone.high_c, f32[32,1536]{1,0:T(8,128)} %constant.39.clone.high_s, bf16[4,512,1536]{2,1,0:T(8,128)(2,1)} %bitcast.13, ...), custom_call_target="tpu_custom_call" | custom-call | tf_op jit(solution)/shard_map/forward/pallas_call | solution.py:128
  10.7 0.0 copy-start.3
  10.7 11.6 %all-to-all-start = ((bf16[32,16,16,128]{3,2,1,0:T(8,128)(2,1)}), bf16[32,16,16,128]{3,2,1,0:T(8,128)(2,1)S(1)}, u32[]{:S(2)}, u32[]{:S(2)}) async-start(bf16[32,16,16,128]{3,2,1,0:T(8,128)(2,1)} %bitcast.12), calls=%async_computation | async-start | bytes 4194304 | tf_op jit(solution)/shard_map/all_to_all | solution.py:391
  23.0 0.1 pad_add_fusion.scalars
  23.0 46.7 %all-to-all-done.x_hbm = bf16[32,16,16,128]{3,2,1,0:T(8,128)(2,1)S(1)} async-done(((bf16[32,16,16,128]{3,2,1,0:T(8,128)(2,1)}), bf16[32,16,16,128]{3,2,1,0:T(8,128)(2,1)S(1)}, u32[]{:S(2)}, u32[]{:S(2)}) %all-to-all-start) | async-done | bytes 2097184 | tf_op jit(solution)/shard_map/all_to_all | solution.py:391
  69.7 1.3 copy-done.6
  71.1 7.2 %spectral.1 = bf16[8192,128]{1,0:T(8,128)(2,1)} custom-call(s32[4]{0:T(128)S(1)} %pad_add_fusion.scalars, f32[16,256]{1,0:T(8,128)S(1)} %copy-done.3, bf16[32,16,16,128]{3,2,1,0:T(8,128)(2,1)} %copy-done.6, bf16[16,512,256]{2,1,0:T(8,128)(2,1)} %l_hbm.1), custom_call_target="tpu_custom_call" | custom-call | tf_op jit(solution)/shard_map/spectral/pallas_call | solution.py:282
  78.3 12.8 %all-to-all-start.1 = ((bf16[128,4,16,128]{3,2,1,0:T(8,128)(2,1)}), bf16[128,4,16,128]{3,2,1,0:T(8,128)(2,1)}, u32[]{:S(2)}, u32[]{:S(2)}) async-start(bf16[128,4,16,128]{3,2,1,0:T(8,128)(2,1)} %bitcast.6), calls=%async_computation.1 | async-start | bytes 4194304 | tf_op jit(solution)/shard_map/all_to_all | solution.py:391
  91.1 8.4 %divide.1 = (bf16[4,128,1536]{2,1,0:T(8,128)(2,1)}, bf16[4,128,1536]{2,1,0:T(8,128)(2,1)}, bf16[4,128,1536]{2,1,0:T(8,128)(2,1)}, bf16[4,128,1536]{2,1,0:T(8,128)(2,1)}) custom-call(s32[4]{0:T(128)} %copy-done.4, bf16[4,512,1536]{2,1,0:T(8,128)(2,1)} %bitcast.14), custom_call_target="tpu_custom_call" | custom-call | flops 10000000000 | bytes 20000000 | tf_op jit(solution)/shard_map/divide/pallas_call | solution.py:176
  99.5 1.5 collective-permute-start
  100.9 2.7 %collective-permute-start.1 = (bf16[4,128,1536]{2,1,0:T(8,128)(2,1)}, bf16[4,128,1536]{2,1,0:T(8,128)(2,1)}, u32[]{:S(2)}, u32[]{:S(2)}) collective-permute-start(bf16[4,128,1536]{2,1,0:T(8,128)(2,1)} %get-tuple-element.21), channel_id=1, source_target_pairs={{0,4},{2,6},{4,0},{6,2},{1,5},{3,7},{5,1},{7,3},{8,12},{10,14},{12... | collective-permute-start | bytes 4718600 | tf_op jit(solution)/shard_map/ppermute | solution.py:410
  103.6 1.5 collective-permute-start.2
  105.1 4.3 %matrices.1 = (bf16[1024,1536]{1,0:T(8,128)(2,1)}, bf16[512,256]{1,0:T(8,128)(2,1)}, bf16[512,512]{1,0:T(8,128)(2,1)}) custom-call(f32[16,32]{1,0:T(8,128)} %modes_ref.3, f32[16,1536]{1,0:T(8,128)} %constant.36.clone.low_c, f32[16,1536]{1,0:T(8,128)} %constant.37.clone.low_s, f32[32,1536]{1,0:T(8,128)} %constant.38.clone.high_c, ...), custom_call_target="tpu_custom_call" | custom-call | flops 1000000000 | bytes 4000000 | tf_op jit(solution)/shard_map/matrices/pallas_call | solution.py:223
  109.4 41.3 %collective-permute-done.rest_1_ = bf16[4,128,1536]{2,1,0:T(8,128)(2,1)} collective-permute-done((bf16[4,128,1536]{2,1,0:T(8,128)(2,1)}, bf16[4,128,1536]{2,1,0:T(8,128)(2,1)}, u32[]{:S(2)}, u32[]{:S(2)}) %collective-permute-start) | collective-permute-done | bytes 1572896 | tf_op jit(solution)/shard_map/ppermute | solution.py:410
  150.8 34.2 %collective-permute-done.1.rest_2_ = bf16[4,128,1536]{2,1,0:T(8,128)(2,1)} collective-permute-done((bf16[4,128,1536]{2,1,0:T(8,128)(2,1)}, bf16[4,128,1536]{2,1,0:T(8,128)(2,1)}, u32[]{:S(2)}, u32[]{:S(2)}) %collective-permute-start.1) | collective-permute-done | bytes 1572896 | tf_op jit(solution)/shard_map/ppermute | solution.py:410
  184.9 0.0 collective-permute-done.2.rest_3_
  185.0 0.9 copy-done.2
  185.9 9.2 %backward.1 = (bf16[64,1536]{1,0:T(8,128)(2,1)S(1)}, bf16[64,1536]{1,0:T(8,128)(2,1)S(1)}) custom-call(s32[4]{0:T(128)S(1)} %copy-done.5, bf16[512,256]{1,0:T(8,128)(2,1)S(1)} %copy-done.2, bf16[32,4,4,16,128]{4,3,2,1,0:T(8,128)(2,1)} %bitcast.7.r_ref, bf16[1024,1536]{1,0:T(8,128)(2,1)} %get-tuple-element.17.ft_ref, bf16[4,128,1536]{2,1,0:T(8,128)(2,1)S(1)} %copy-done, ...), custom_call_target="tpu_custom_call" | custom-call | tf_op jit(solution)/shard_map/backward/pallas_call | solution.py:346
  195.1 5.4 %collective-permute-start.3 = (bf16[64,1536]{1,0:T(8,128)(2,1)S(1)}, bf16[64,1536]{1,0:T(8,128)(2,1)S(1)}, u32[]{:S(2)}, u32[]{:S(2)}) collective-permute-start(bf16[64,1536]{1,0:T(8,128)(2,1)S(1)} %get-tuple-element.24), channel_id=1, source_target_pairs={{0,1},{1,0},{2,3},{3,2},{4,5},{5,4},{6,7},{7,6},{8,9},{9,8},{10,11... | collective-permute-start | bytes 589832 | tf_op jit(solution)/shard_map/ppermute | solution.py:416
  200.5 4.5 %collective-permute-done.3 = bf16[64,1536]{1,0:T(8,128)(2,1)S(1)} collective-permute-done((bf16[64,1536]{1,0:T(8,128)(2,1)S(1)}, bf16[64,1536]{1,0:T(8,128)(2,1)S(1)}, u32[]{:S(2)}, u32[]{:S(2)}) %collective-permute-start.3) | collective-permute-done | bytes 196640 | tf_op jit(solution)/shard_map/ppermute | solution.py:416
  205.0 0.1 multiply_convert_fusion
  205.1 0.1 broadcast_in_dim.2
  205.2 25.5 %all_to_all.15 = bf16[8,64,1536]{2,1,0:T(8,128)(2,1)S(1)} all-to-all(bf16[8,64,1536]{2,1,0:T(8,128)(2,1)S(1)} %broadcast_in_dim.2), channel_id=1, replica_groups=mesh['space_0'=4,'space_1'=4,'space_2'=2,'mem_y'=4,'mem_z'=2] {'mem_y','..., dimensions={0} | all-to-all | bytes 3145728 | tf_op jit(solution)/shard_map/all_to_all | solution.py:391
  230.7 2.6 %place.1 = bf16[512,1536]{1,0:T(8,128)(2,1)} custom-call(bf16[512,512]{1,0:T(8,128)(2,1)S(1)} %copy-done.1, bf16[512,1536]{1,0:T(8,128)(2,1)S(1)} %bitcast.11), custom_call_target="tpu_custom_call" | custom-call | tf_op jit(solution)/shard_map/place/pallas_call | solution.py:376
  (12 shorter events, 0.0 us)
Async XLA Ops:
  10.7 60.4 %copy-start.3 = (f32[16,256]{1,0:T(8,128)S(1)}, f32[16,256]{1,0:T(8,128)}, u32[]{:S(2)}) copy-start(f32[16,256]{1,0:T(8,128)} %spectrum_ref.1) | copy-start | bytes 49156
  10.7 59.0 %all-to-all-start = ((bf16[32,16,16,128]{3,2,1,0:T(8,128)(2,1)}), bf16[32,16,16,128]{3,2,1,0:T(8,128)(2,1)S(1)}, u32[]{:S(2)}, u32[]{:S(2)}) async-start(bf16[32,16,16,128]{3,2,1,0:T(8,128)(2,1)} %bitcast.12), calls=%async_computation | async-start | bytes 4194304 | tf_op jit(solution)/shard_map/all_to_all | solution.py:391
  23.0 55.3 %copy-start.4 = (s32[4]{0:T(128)}, s32[4]{0:T(128)S(1)}, u32[]{:S(2)}) copy-start(s32[4]{0:T(128)S(1)} %pad_add_fusion.scalars) | copy-start | bytes 52
  69.7 1.3 copy-start.6
  78.3 106.6 %all-to-all-start.1 = ((bf16[128,4,16,128]{3,2,1,0:T(8,128)(2,1)}), bf16[128,4,16,128]{3,2,1,0:T(8,128)(2,1)}, u32[]{:S(2)}, u32[]{:S(2)}) async-start(bf16[128,4,16,128]{3,2,1,0:T(8,128)(2,1)} %bitcast.6), calls=%async_computation.1 | async-start | bytes 4194304 | tf_op jit(solution)/shard_map/all_to_all | solution.py:391
  99.5 51.3 %collective-permute-start = (bf16[4,128,1536]{2,1,0:T(8,128)(2,1)}, bf16[4,128,1536]{2,1,0:T(8,128)(2,1)}, u32[]{:S(2)}, u32[]{:S(2)}) collective-permute-start(bf16[4,128,1536]{2,1,0:T(8,128)(2,1)} %get-tuple-element.20), channel_id=1, source_target_pairs={{0,2},{2,4},{4,6},{6,0},{1,3},{3,5},{5,7},{7,1},{8,10},{10,12},{12... | collective-permute-start | bytes 4718600 | tf_op jit(solution)/shard_map/ppermute | solution.py:410
  100.9 84.0 %collective-permute-start.1 = (bf16[4,128,1536]{2,1,0:T(8,128)(2,1)}, bf16[4,128,1536]{2,1,0:T(8,128)(2,1)}, u32[]{:S(2)}, u32[]{:S(2)}) collective-permute-start(bf16[4,128,1536]{2,1,0:T(8,128)(2,1)} %get-tuple-element.21), channel_id=1, source_target_pairs={{0,4},{2,6},{4,0},{6,2},{1,5},{3,7},{5,1},{7,3},{8,12},{10,14},{12... | collective-permute-start | bytes 4718600 | tf_op jit(solution)/shard_map/ppermute | solution.py:410
  103.6 81.3 %copy-start = (bf16[4,128,1536]{2,1,0:T(8,128)(2,1)S(1)}, bf16[4,128,1536]{2,1,0:T(8,128)(2,1)}, u32[]{:S(2)}) copy-start(bf16[4,128,1536]{2,1,0:T(8,128)(2,1)} %get-tuple-element.19.rest_0_) | copy-start | bytes 4718596
  103.6 81.3 %copy-start.5 = (s32[4]{0:T(128)S(1)}, s32[4]{0:T(128)}, u32[]{:S(2)}) copy-start(s32[4]{0:T(128)} %copy-done.4) | copy-start | bytes 52
  103.6 81.3 %collective-permute-start.2 = (bf16[4,128,1536]{2,1,0:T(8,128)(2,1)}, bf16[4,128,1536]{2,1,0:T(8,128)(2,1)}, u32[]{:S(2)}, u32[]{:S(2)}) collective-permute-start(bf16[4,128,1536]{2,1,0:T(8,128)(2,1)} %get-tuple-element.22), channel_id=1, source_target_pairs={{0,6},{2,0},{4,2},{6,4},{1,7},{3,1},{5,3},{7,5},{8,14},{10,8},{12,... | collective-permute-start | bytes 4718600 | tf_op jit(solution)/shard_map/ppermute | solution.py:410
  185.0 1.0 copy-start.2
  195.1 9.9 %collective-permute-start.3 = (bf16[64,1536]{1,0:T(8,128)(2,1)S(1)}, bf16[64,1536]{1,0:T(8,128)(2,1)S(1)}, u32[]{:S(2)}, u32[]{:S(2)}) collective-permute-start(bf16[64,1536]{1,0:T(8,128)(2,1)S(1)} %get-tuple-element.24), channel_id=1, source_target_pairs={{0,1},{1,0},{2,3},{3,2},{4,5},{5,4},{6,7},{7,6},{8,9},{9,8},{10,11... | collective-permute-start | bytes 589832 | tf_op jit(solution)/shard_map/ppermute | solution.py:416
  205.2 25.5 %copy-start.1 = (bf16[512,512]{1,0:T(8,128)(2,1)S(1)}, bf16[512,512]{1,0:T(8,128)(2,1)}, u32[]{:S(2)}) copy-start(bf16[512,512]{1,0:T(8,128)(2,1)} %get-tuple-element.15.order_ref) | copy-start | bytes 1572868

commit v3 on v2

--- a/solution.py
+++ b/solution.py
@@ -151,40 +151,34 @@
     )
 
 
-def divide_kernel(scalars, e_ref, *rest, rows):
-    *out_refs, perm = rest
-    parts = len(out_refs)
-    share = out_refs[0].shape[1]
+def divide_kernel(scalars, e_ref, out_ref, perm, *, rows, parts, up):
     per = rows // parts
 
     @pl.when(pl.program_id(0) == 0)
     def _():
         row = iota2(perm.shape, 0)
-        part = rest_of(scalars[2] + over(row, share), parts)
-        level = over(rest_of(row, share), per)
-        perm[...] = one_hot(iota2(perm.shape, 1) == level * rows + part * per + rest_of(row, per))
-
-    moved = jnp.dot(perm[...], e_ref[0], preferred_element_type=F32).astype(BF16)
-    for d, out_ref in enumerate(out_refs):
-        out_ref[0] = moved[d * share : (d + 1) * share]
-
-
-def divide(scalars, ensemble, parts):
+        part = rest_of(scalars[2] + up, parts)
+        perm[...] = one_hot(iota2(perm.shape, 1) == over(row, per) * rows + part * per + rest_of(row, per))
+
+    out_ref[0] = jnp.dot(perm[...], e_ref[0], preferred_element_type=F32).astype(BF16)
+
+
+def divide(scalars, ensemble, parts, up):
     members, levels, rows, lons = ensemble.shape
     height = levels * rows
     share = height // parts
     return pl.pallas_call(
-        functools.partial(divide_kernel, rows=rows),
+        functools.partial(divide_kernel, rows=rows, parts=parts, up=up),
         grid_spec=pltpu.PrefetchScalarGridSpec(
             num_scalar_prefetch=1,
             grid=(members,),
             in_specs=[pl.BlockSpec((1, height, lons), lambda k, _: (k, 0, 0))],
-            out_specs=[pl.BlockSpec((1, share, lons), lambda k, _: (k, 0, 0))] * parts,
-            scratch_shapes=[pltpu.VMEM((height, height), BF16)],
+            out_specs=pl.BlockSpec((1, share, lons), lambda k, _: (k, 0, 0)),
+            scratch_shapes=[pltpu.VMEM((share, height), BF16)],
         ),
-        out_shape=[jax.ShapeDtypeStruct((members, share, lons), BF16)] * parts,
+        out_shape=jax.ShapeDtypeStruct((members, share, lons), BF16),
         compiler_params=pltpu.CompilerParams(vmem_limit_bytes=62 * 2**20),
-        cost_estimate=pl.CostEstimate(flops=10**10, bytes_accessed=2 * 10**7, transcendentals=0),
+        cost_estimate=pl.CostEstimate(flops=25 * 10**8, bytes_accessed=8 * 10**6, transcendentals=0),
         name="divide",
     )(scalars, ensemble.reshape(members, height, lons))
 
@@ -405,9 +399,11 @@
     zonal = forward(modes, ensemble, vector)
     arrived = swap(zonal.reshape(sources, waves, rows, lanes), SPACE)
     held, _ = lax.optimization_barrier((ensemble, zonal))
-    pieces = list(divide(scalars, held, parts))
-    for d in range(1, parts):
-        pieces[d] = lax.ppermute(pieces[d], "mem_y", [(i, (i + d) % parts) for i in range(parts)])
+    pieces = [None] * parts
+    for d in (2, 1, 3, 0):
+        pieces[d] = divide(scalars, held, parts, d)
+        if d:
+            pieces[d] = lax.ppermute(pieces[d], "mem_y", [(i, (i + d) % parts) for i in range(parts)])
     fourier, lift, order = matrices(modes, members, rows, parts, halves)
     synthesis = spectral(scalars, spectrum, arrived, legendre)
     returned = swap(synthesis.reshape(sources * parts, quarter, waves, lanes), SPACE + ("mem_y",))

time: 234 us -> 237 us (1.013)
  waiting for transfers between devices: 127 us -> 111 us
  Pallas kernels: 42.4 us -> 57.6 us
  starting transfers between devices: 35.4 us -> 37.8 us
    pallas_call x1 -> x4, Pallas kernels: 8.39 us -> 23.8 us  [divide(): pl.pallas_call(functools.partial(divide_kernel, rows=rows, parts=parts, u...]
    ppermute x3, waiting for transfers between devices: 75.5 us -> 60.6 us  [on_device(): lax.ppermute(pieces[d], 'mem_y', [(i, (i + d) % parts) for i in range(par...]
    ppermute x1, starting transfers between devices: 5.41 us -> 7.81 us  [on_device(): came = lax.ppermute(sent, 'mem_z', [(0, 1), (1, 0)])]
  transfers between devices with their start and end apart: 6 -> 6, of which waited for: 4 -> 5; matrix products, arithmetic and copies ran while one was open for 0% -> 0% of each run, Pallas kernels for 5% -> 12%
where the time goes in v3:
time: 237 us; the launch traced here: 236 us
  waiting for transfers between devices  111 us (47%)
  Pallas kernels  57.6 us (24%)
  starting transfers between devices  37.8 us (16%)
  blocking collectives  25.6 us (11%)
  local copies, waits for them, and re-layouts  2.88 us (1%)
    ppermute x3, waiting for transfers between devices, on_device(): lax.ppermute(pieces[d], 'mem_y', [(i, (i + d) % parts) for i in range(par...  60.6 us
    all_to_all x2, waiting for transfers between devices, swap(): return lax.all_to_all(blocks, axes, 0, 0, tiled=True)  46.7 us
    all_to_all x1, blocking collectives, swap(): return lax.all_to_all(blocks, axes, 0, 0, tiled=True)  25.6 us
    all_to_all x2, starting transfers between devices, swap(): return lax.all_to_all(blocks, axes, 0, 0, tiled=True)  24.4 us
    pallas_call x4, Pallas kernels, divide(): pl.pallas_call(functools.partial(divide_kernel, rows=rows, parts=parts, u...  23.8 us
    pallas_call x1, Pallas kernels, forward(): pl.pallas_call(forward_kernel, in_specs=[whole] * 5 + [outside] * 2, out_...  10.7 us
    pallas_call x1, Pallas kernels, backward(): pl.pallas_call(backward_kernel, grid_spec=pltpu.PrefetchScalarGridSpec(nu...  9.08 us
    ppermute x1, starting transfers between devices, on_device(): came = lax.ppermute(sent, 'mem_z', [(0, 1), (1, 0)])  7.81 us
  transfers between devices with their start and end apart: 6, of which 5 were waited for; matrix products, arithmetic and copies ran while one was open for 0% of the time, Pallas kernels for 12%

profile of v3, /device:TPU:2, one launch (start us, length us, event | category | flops | bytes accessed | tf_op | source)
XLA Modules:
  0.0 236.2 jit_solution(18417862017094176294)
XLA Ops:
  0.0 10.7 %forward.1 = bf16[8192,128]{1,0:T(8,128)(2,1)} custom-call(f32[16,32]{1,0:T(8,128)} %modes_ref.3, f32[16,1536]{1,0:T(8,128)} %constant.36.clone.low_c, f32[16,1536]{1,0:T(8,128)} %constant.37.clone.low_s, f32[32,1536]{1,0:T(8,128)} %constant.38.clone.high_c, f32[32,1536]{1,0:T(8,128)} %constant.39.clone.high_s, bf16[4,512,1536]{2,1,0:T(8,128)(2,1)} %bitcast.13, ...), custom_call_target="tpu_custom_call" | custom-call | tf_op jit(solution)/shard_map/forward/pallas_call | solution.py:128
  10.7 11.6 %all-to-all-start = ((bf16[32,16,16,128]{3,2,1,0:T(8,128)(2,1)}), bf16[32,16,16,128]{3,2,1,0:T(8,128)(2,1)S(1)}, u32[]{:S(2)}, u32[]{:S(2)}) async-start(bf16[32,16,16,128]{3,2,1,0:T(8,128)(2,1)} %bitcast.12), calls=%async_computation | async-start | bytes 4194304 | tf_op jit(solution)/shard_map/all_to_all | solution.py:385
  23.0 46.7 %all-to-all-done.x_hbm = bf16[32,16,16,128]{3,2,1,0:T(8,128)(2,1)S(1)} async-done(((bf16[32,16,16,128]{3,2,1,0:T(8,128)(2,1)}), bf16[32,16,16,128]{3,2,1,0:T(8,128)(2,1)S(1)}, u32[]{:S(2)}, u32[]{:S(2)}) %all-to-all-start) | async-done | bytes 2097184 | tf_op jit(solution)/shard_map/all_to_all | solution.py:385
  69.7 1.3 copy-done.6
  71.0 7.2 %spectral.1 = bf16[8192,128]{1,0:T(8,128)(2,1)} custom-call(s32[4]{0:T(128)S(1)} %pad_add_fusion.scalars, f32[16,256]{1,0:T(8,128)S(1)} %copy-done.3, bf16[32,16,16,128]{3,2,1,0:T(8,128)(2,1)} %copy-done.6, bf16[16,512,256]{2,1,0:T(8,128)(2,1)} %l_hbm.1), custom_call_target="tpu_custom_call" | custom-call | tf_op jit(solution)/shard_map/spectral/pallas_call | solution.py:276
  78.3 12.8 %all-to-all-start.1 = ((bf16[128,4,16,128]{3,2,1,0:T(8,128)(2,1)}), bf16[128,4,16,128]{3,2,1,0:T(8,128)(2,1)}, u32[]{:S(2)}, u32[]{:S(2)}) async-start(bf16[128,4,16,128]{3,2,1,0:T(8,128)(2,1)} %bitcast.6), calls=%async_computation.1 | async-start | bytes 4194304 | tf_op jit(solution)/shard_map/all_to_all | solution.py:385
  91.1 5.9 %divide.5 = bf16[4,128,1536]{2,1,0:T(8,128)(2,1)} custom-call(s32[4]{0:T(128)} %copy-done.4, bf16[4,512,1536]{2,1,0:T(8,128)(2,1)} %bitcast.14), custom_call_target="tpu_custom_call" | custom-call | flops 2500000000 | bytes 8000000 | tf_op jit(solution)/shard_map/divide/pallas_call | solution.py:170
  97.0 1.5 collective-permute-start
  98.4 5.9 %divide.6 = bf16[4,128,1536]{2,1,0:T(8,128)(2,1)} custom-call(s32[4]{0:T(128)} %copy-done.4, bf16[4,512,1536]{2,1,0:T(8,128)(2,1)} %bitcast.15), custom_call_target="tpu_custom_call" | custom-call | flops 2500000000 | bytes 8000000 | tf_op jit(solution)/shard_map/divide/pallas_call | solution.py:170
  104.3 2.7 %collective-permute-start.1 = (bf16[4,128,1536]{2,1,0:T(8,128)(2,1)}, bf16[4,128,1536]{2,1,0:T(8,128)(2,1)}, u32[]{:S(2)}, u32[]{:S(2)}) collective-permute-start(bf16[4,128,1536]{2,1,0:T(8,128)(2,1)} %divide.6), channel_id=1, source_target_pairs={{0,4},{2,6},{4,0},{6,2},{1,5},{3,7},{5,1},{7,3},{8,12},{10,14},{12... | collective-permute-start | bytes 4718600 | tf_op jit(solution)/shard_map/ppermute | solution.py:406
  107.0 5.9 %divide.7 = bf16[4,128,1536]{2,1,0:T(8,128)(2,1)} custom-call(s32[4]{0:T(128)} %copy-done.4, bf16[4,512,1536]{2,1,0:T(8,128)(2,1)} %bitcast.16), custom_call_target="tpu_custom_call" | custom-call | flops 2500000000 | bytes 8000000 | tf_op jit(solution)/shard_map/divide/pallas_call | solution.py:170
  112.9 1.5 collective-permute-start.2
  114.4 4.3 %matrices.1 = (bf16[1024,1536]{1,0:T(8,128)(2,1)}, bf16[512,256]{1,0:T(8,128)(2,1)}, bf16[512,512]{1,0:T(8,128)(2,1)}) custom-call(f32[16,32]{1,0:T(8,128)} %modes_ref.3, f32[16,1536]{1,0:T(8,128)} %constant.36.clone.low_c, f32[16,1536]{1,0:T(8,128)} %constant.37.clone.low_s, f32[32,1536]{1,0:T(8,128)} %constant.38.clone.high_c, ...), custom_call_target="tpu_custom_call" | custom-call | flops 1000000000 | bytes 4000000 | tf_op jit(solution)/shard_map/matrices/pallas_call | solution.py:217
  118.7 6.0 %divide.4.rest_0_ = bf16[4,128,1536]{2,1,0:T(8,128)(2,1)} custom-call(s32[4]{0:T(128)} %copy-done.4, bf16[4,512,1536]{2,1,0:T(8,128)(2,1)} %bitcast.17), custom_call_target="tpu_custom_call" | custom-call | flops 2500000000 | bytes 8000000 | tf_op jit(solution)/shard_map/divide/pallas_call | solution.py:170
  124.8 25.5 %collective-permute-done.rest_1_ = bf16[4,128,1536]{2,1,0:T(8,128)(2,1)S(1)} collective-permute-done((bf16[4,128,1536]{2,1,0:T(8,128)(2,1)}, bf16[4,128,1536]{2,1,0:T(8,128)(2,1)S(1)}, u32[]{:S(2)}, u32[]{:S(2)}) %collective-permute-start) | collective-permute-done | bytes 1572896 | tf_op jit(solution)/shard_map/ppermute | solution.py:406
  150.3 33.8 %collective-permute-done.1.rest_2_ = bf16[4,128,1536]{2,1,0:T(8,128)(2,1)} collective-permute-done((bf16[4,128,1536]{2,1,0:T(8,128)(2,1)}, bf16[4,128,1536]{2,1,0:T(8,128)(2,1)}, u32[]{:S(2)}, u32[]{:S(2)}) %collective-permute-start.1) | collective-permute-done | bytes 1572896 | tf_op jit(solution)/shard_map/ppermute | solution.py:406
  184.1 1.3 collective-permute-done.2.rest_3_
  185.4 1.4 copy-done
  186.8 9.1 %backward.1 = (bf16[64,1536]{1,0:T(8,128)(2,1)S(1)}, bf16[64,1536]{1,0:T(8,128)(2,1)S(1)}) custom-call(s32[4]{0:T(128)S(1)} %copy-done.5, bf16[512,256]{1,0:T(8,128)(2,1)S(1)} %copy-done.2, bf16[32,4,4,16,128]{4,3,2,1,0:T(8,128)(2,1)} %bitcast.7.r_ref, bf16[1024,1536]{1,0:T(8,128)(2,1)} %get-tuple-element.13.ft_ref, bf16[4,128,1536]{2,1,0:T(8,128)(2,1)S(1)} %copy-done, ...), custom_call_target="tpu_custom_call" | custom-call | tf_op jit(solution)/shard_map/backward/pallas_call | solution.py:340
  195.9 7.8 %collective-permute-start.3 = (bf16[64,1536]{1,0:T(8,128)(2,1)S(1)}, bf16[64,1536]{1,0:T(8,128)(2,1)S(1)}, u32[]{:S(2)}, u32[]{:S(2)}) collective-permute-start(bf16[64,1536]{1,0:T(8,128)(2,1)S(1)} %get-tuple-element.16), channel_id=1, source_target_pairs={{0,1},{1,0},{2,3},{3,2},{4,5},{5,4},{6,7},{7,6},{8,9},{9,8},{10,11... | collective-permute-start | bytes 589832 | tf_op jit(solution)/shard_map/ppermute | solution.py:412
  203.7 4.1 %collective-permute-done.3 = bf16[64,1536]{1,0:T(8,128)(2,1)S(1)} collective-permute-done((bf16[64,1536]{1,0:T(8,128)(2,1)S(1)}, bf16[64,1536]{1,0:T(8,128)(2,1)S(1)}, u32[]{:S(2)}, u32[]{:S(2)}) %collective-permute-start.3) | collective-permute-done | bytes 196640 | tf_op jit(solution)/shard_map/ppermute | solution.py:412
  207.9 0.1 broadcast_in_dim.2
  208.1 25.6 %all_to_all.15 = bf16[8,64,1536]{2,1,0:T(8,128)(2,1)S(1)} all-to-all(bf16[8,64,1536]{2,1,0:T(8,128)(2,1)S(1)} %broadcast_in_dim.2), channel_id=1, replica_groups=mesh['space_0'=4,'space_1'=4,'space_2'=2,'mem_y'=4,'mem_z'=2] {'mem_y','..., dimensions={0} | all-to-all | bytes 3145728 | tf_op jit(solution)/shard_map/all_to_all | solution.py:385
  233.6 2.6 %place.1 = bf16[512,1536]{1,0:T(8,128)(2,1)} custom-call(bf16[512,512]{1,0:T(8,128)(2,1)S(1)} %copy-done.1, bf16[512,1536]{1,0:T(8,128)(2,1)S(1)} %bitcast.11), custom_call_target="tpu_custom_call" | custom-call | tf_op jit(solution)/shard_map/place/pallas_call | solution.py:370
  (15 shorter events, 0.2 us)
Async XLA Ops:
  10.7 60.4 %copy-start.3 = (f32[16,256]{1,0:T(8,128)S(1)}, f32[16,256]{1,0:T(8,128)}, u32[]{:S(2)}) copy-start(f32[16,256]{1,0:T(8,128)} %spectrum_ref.1) | copy-start | bytes 49156
  10.7 59.0 %all-to-all-start = ((bf16[32,16,16,128]{3,2,1,0:T(8,128)(2,1)}), bf16[32,16,16,128]{3,2,1,0:T(8,128)(2,1)S(1)}, u32[]{:S(2)}, u32[]{:S(2)}) async-start(bf16[32,16,16,128]{3,2,1,0:T(8,128)(2,1)} %bitcast.12), calls=%async_computation | async-start | bytes 4194304 | tf_op jit(solution)/shard_map/all_to_all | solution.py:385
  23.0 55.2 %copy-start.4 = (s32[4]{0:T(128)}, s32[4]{0:T(128)S(1)}, u32[]{:S(2)}) copy-start(s32[4]{0:T(128)S(1)} %pad_add_fusion.scalars) | copy-start | bytes 52
  69.7 1.3 copy-start.6
  78.3 107.1 %all-to-all-start.1 = ((bf16[128,4,16,128]{3,2,1,0:T(8,128)(2,1)}), bf16[128,4,16,128]{3,2,1,0:T(8,128)(2,1)}, u32[]{:S(2)}, u32[]{:S(2)}) async-start(bf16[128,4,16,128]{3,2,1,0:T(8,128)(2,1)} %bitcast.6), calls=%async_computation.1 | async-start | bytes 4194304 | tf_op jit(solution)/shard_map/all_to_all | solution.py:385
  97.0 53.3 %collective-permute-start = (bf16[4,128,1536]{2,1,0:T(8,128)(2,1)}, bf16[4,128,1536]{2,1,0:T(8,128)(2,1)S(1)}, u32[]{:S(2)}, u32[]{:S(2)}) collective-permute-start(bf16[4,128,1536]{2,1,0:T(8,128)(2,1)} %divide.5), channel_id=1, source_target_pairs={{0,2},{2,4},{4,6},{6,0},{1,3},{3,5},{5,7},{7,1},{8,10},{10,12},{12... | collective-permute-start | bytes 4718600 | tf_op jit(solution)/shard_map/ppermute | solution.py:406
  104.3 79.8 %collective-permute-start.1 = (bf16[4,128,1536]{2,1,0:T(8,128)(2,1)}, bf16[4,128,1536]{2,1,0:T(8,128)(2,1)}, u32[]{:S(2)}, u32[]{:S(2)}) collective-permute-start(bf16[4,128,1536]{2,1,0:T(8,128)(2,1)} %divide.6), channel_id=1, source_target_pairs={{0,4},{2,6},{4,0},{6,2},{1,5},{3,7},{5,1},{7,3},{8,12},{10,14},{12... | collective-permute-start | bytes 4718600 | tf_op jit(solution)/shard_map/ppermute | solution.py:406
  112.9 72.5 %collective-permute-start.2 = (bf16[4,128,1536]{2,1,0:T(8,128)(2,1)}, bf16[4,128,1536]{2,1,0:T(8,128)(2,1)}, u32[]{:S(2)}, u32[]{:S(2)}) collective-permute-start(bf16[4,128,1536]{2,1,0:T(8,128)(2,1)} %divide.7), channel_id=1, source_target_pairs={{0,6},{2,0},{4,2},{6,4},{1,7},{3,1},{5,3},{7,5},{8,14},{10,8},{12,... | collective-permute-start | bytes 4718600 | tf_op jit(solution)/shard_map/ppermute | solution.py:406
  118.7 66.7 %copy-start.2 = (bf16[512,256]{1,0:T(8,128)(2,1)S(1)}, bf16[512,256]{1,0:T(8,128)(2,1)}, u32[]{:S(2)}) copy-start(bf16[512,256]{1,0:T(8,128)(2,1)} %get-tuple-element.12.kl_ref) | copy-start | bytes 786436
  118.7 66.7 %copy-start.5 = (s32[4]{0:T(128)S(1)}, s32[4]{0:T(128)}, u32[]{:S(2)}) copy-start(s32[4]{0:T(128)} %copy-done.4) | copy-start | bytes 52
  185.4 1.4 copy-start
  195.9 11.9 %collective-permute-start.3 = (bf16[64,1536]{1,0:T(8,128)(2,1)S(1)}, bf16[64,1536]{1,0:T(8,128)(2,1)S(1)}, u32[]{:S(2)}, u32[]{:S(2)}) collective-permute-start(bf16[64,1536]{1,0:T(8,128)(2,1)S(1)} %get-tuple-element.16), channel_id=1, source_target_pairs={{0,1},{1,0},{2,3},{3,2},{4,5},{5,4},{6,7},{7,6},{8,9},{9,8},{10,11... | collective-permute-start | bytes 589832 | tf_op jit(solution)/shard_map/ppermute | solution.py:412
  208.1 25.6 %copy-start.1 = (bf16[512,512]{1,0:T(8,128)(2,1)S(1)}, bf16[512,512]{1,0:T(8,128)(2,1)}, u32[]{:S(2)}) copy-start(bf16[512,512]{1,0:T(8,128)(2,1)} %get-tuple-element.11.order_ref) | copy-start | bytes 1572868
